TPU v7x, 32 devices: a whole 2x2x4 slice. The times are simulated.
32 devices in a mesh: rows: 16 (over z, x, core), cols: 2 (over y).
Axes of the slice: x: 2, y: 2, z: 4, core: 2. Of those that a mesh axis runs over, the one named last changes fastest.
Arguments:
- kets: float32 [16, 4, 32], P('rows', 'cols'), may hold values from -3 to 3
- left_maps: float32 [2, 16, 4, 96, 384], P(None, 'rows', 'cols'), may hold values from -0.3125 to 0.3125
- right_maps: float32 [2, 16, 4, 96, 384], P(None, 'rows', 'cols'), may hold values from -0.3125 to 0.3125
- top_edge: float32 [4, 96, 384], P('cols'), may hold values from -6 to 6
- bottom_edge: float32 [4, 96, 384], P('cols'), may hold values from -6 to 6
- left_edge: float32 [16, 96, 384], P('rows'), may hold values from -6 to 6
- right_edge: float32 [16, 96, 384], P('rows'), may hold values from -6 to 6
- term_rows: int32 [16], replicated, may hold values from 0 to 15
- term_bonds: int32 [16], replicated, may hold values from 0 to 2
- term_ops: int32 [16], replicated, may hold values from 0 to 3
- operators: float32 [4, 16], replicated, may hold values from -6 to 6
Outputs:
- top_out: float32 [16, 4, 96, 384], P('rows', 'cols')
- bottom_out: float32 [16, 4, 96, 384], P('rows', 'cols')
- energies: float32 [16], replicated
Inputs may be any that keep to these rules, and one draw needn't show every extreme that they name: Term t acts on the bond between columns term_bonds[t] and term_bonds[t] + 1 of row term_rows[t].
All inputs are finite; a program needn't handle non-finite values.
Results may differ from a plain program's by a relative error of at most 0.0003.
Values sent between devices are 32-bit elements; how exact they have to be, the bound alone decides.
A program may use at most 64 MiB of HBM per device.

v0:
```python
import jax
import jax.numpy as jnp
from jax import lax
from jax.sharding import PartitionSpec as P

D = 2
D2 = 4
PHYS = 2
CHI = 96
OPS = 4
TERMS = 16


EPSILON = 1e-06
PRECISION_HIGH = lax.Precision.HIGHEST


def shifted(value, axis, steps):
    count = lax.axis_size(axis)
    initial, last = (max(0, -steps), min(count, count - steps))
    return lax.ppermute(value, axis, [(source, source + steps) for source in range(initial, last)])


def product(pattern, former, latter):
    return jnp.einsum(
        pattern, former, latter, precision=PRECISION_HIGH, preferred_element_type=jnp.float32
    )


def normalize(values):
    return values / jnp.sqrt(jnp.mean(values * values) + EPSILON)


def select_at(values, position):
    return lax.dynamic_index_in_dim(values, position, 0, keepdims=False)


def pair_layers(ket_flat):
    tensor = ket_flat.reshape(PHYS, D, D, D, D)
    doubled = product("pabcd,pefgh->aebfcgdh", tensor, tensor)
    return doubled.reshape(D2, D2, D2, D2)


def open_layers(ket_flat):
    tensor = ket_flat.reshape(PHYS, D, D, D, D)
    doubled = product("pabcd,qefgh->pqaebfcgdh", tensor, tensor)
    return doubled.reshape(PHYS * PHYS, D2, D2, D2, D2)


def pair_diagonal():
    matched = jnp.arange(PHYS)[:, None] == jnp.arange(PHYS)[None, :]
    return jnp.where(matched, 1.0, 0.0).astype(jnp.float32).reshape(PHYS * PHYS)


def absorb_down(boundary, layers, left_map, right_map):
    above_col = boundary.reshape(CHI, D2, CHI)
    left_three = left_map.reshape(CHI, CHI, D2)
    right_three = right_map.reshape(CHI, CHI, D2)
    joined = product("aub,cbr->aurc", above_col, right_three)
    through = product("aurc,uldr->aldc", joined, layers)
    renewed = product("xal,aldc->xdc", left_three, through)
    return normalize(renewed.reshape(CHI, D2 * CHI))


def absorb_up(boundary, layers, left_map, right_map):
    below_col = boundary.reshape(CHI, D2, CHI)
    left_three = left_map.reshape(CHI, CHI, D2)
    right_three = right_map.reshape(CHI, CHI, D2)
    joined = product("adb,cbr->adrc", below_col, right_three)
    through = product("adrc,uldr->aluc", joined, layers)
    renewed = product("xal,aluc->xuc", left_three, through)
    return normalize(renewed.reshape(CHI, D2 * CHI))


def left_core(environ, layers, above_col, below_col):
    env_three = environ.reshape(CHI, D2, CHI)
    upper_three = above_col.reshape(CHI, D2, CHI)
    lower_three = below_col.reshape(CHI, D2, CHI)
    step_one = product("alb,aux->lbux", env_three, upper_three)
    step_two = product("lbux,uldr->bxdr", step_one, layers)
    return product("bxdr,bdy->xry", step_two, lower_three).reshape(CHI, D2 * CHI)


def right_core(environ, layers, above_col, below_col):
    env_three = environ.reshape(CHI, D2, CHI)
    upper_three = above_col.reshape(CHI, D2, CHI)
    lower_three = below_col.reshape(CHI, D2, CHI)
    step_one = product("xry,aux->ryau", env_three, upper_three)
    step_two = product("ryau,uldr->yald", step_one, layers)
    return product("yald,bdy->alb", step_two, lower_three).reshape(CHI, D2 * CHI)


def side_step(core_map, environ, ket_flat, layers, above_col, below_col, wanted):

    def with_open(unused):
        opened = lax.map(
            lambda single: core_map(environ, single, above_col, below_col), open_layers(ket_flat)
        )
        closed = jnp.sum(pair_diagonal()[:, None, None] * opened, axis=0)
        return (opened, normalize(closed))

    def without_open(unused):
        empty_open = jnp.zeros((PHYS * PHYS, CHI, D2 * CHI), jnp.float32)
        return (empty_open, normalize(core_map(environ, layers, above_col, below_col)))

    return lax.cond(wanted, with_open, without_open, 0)


def shards(
    kets,
    left_maps,
    right_maps,
    top_edge,
    bottom_edge,
    left_edge,
    right_edge,
    term_rows,
    term_bonds,
    term_ops,
    operators,
):
    row_count = lax.axis_size("rows")
    row_place = lax.axis_index("rows")
    col_count = lax.axis_size("cols")
    col_place = lax.axis_index("cols")
    local_rows = kets.shape[0]
    local_cols = kets.shape[1]
    layers = jax.vmap(jax.vmap(pair_layers))(kets)
    column_shape = (CHI, D2 * CHI)
    blank_column = jnp.zeros(column_shape, jnp.float32)

    def run_down(source, column):
        current = source
        current = absorb_down(
            current,
            select_at(layers[0], column),
            select_at(left_maps[0, 0], column),
            select_at(right_maps[0, 0], column),
        )
        columns_out = [current]
        return jnp.stack(columns_out)

    def run_up(source, column):
        columns_out = [None] * local_rows
        current = source
        for local_row in reversed(range(local_rows)):
            current = absorb_up(
                current,
                select_at(layers[local_row], column),
                select_at(left_maps[1, local_row], column),
                select_at(right_maps[1, local_row], column),
            )
            columns_out[local_row] = current
        return jnp.stack(columns_out)

    def pipe_step(step_number, carried):
        from_above, from_below, enter_top, leave_top, enter_bottom, leave_bottom = carried
        slot_top = step_number - row_place
        column_top = jnp.clip(slot_top, 0, local_cols - 1)
        source_top = jnp.where(row_place == 0, select_at(top_edge, column_top), from_above)

        def down_live(stores):
            renewed = run_down(source_top, column_top)
            entered = lax.dynamic_update_index_in_dim(stores[0], source_top, column_top, 0)
            left_now = lax.dynamic_update_index_in_dim(stores[1], renewed, column_top, 1)
            return (entered, left_now, renewed[local_rows - 1])

        def down_spare(stores):
            return (stores[0], stores[1], blank_column)

        live_top = (slot_top >= 0) & (slot_top < local_cols)
        enter_top, leave_top, send_down = lax.cond(
            live_top, down_live, down_spare, (enter_top, leave_top)
        )
        slot_bottom = step_number - (row_count - 1 - row_place)
        column_bottom = jnp.clip(slot_bottom, 0, local_cols - 1)
        source_bottom = jnp.where(
            row_place == row_count - 1, select_at(bottom_edge, column_bottom), from_below
        )

        def up_live(stores):
            renewed = run_up(source_bottom, column_bottom)
            entered = lax.dynamic_update_index_in_dim(stores[0], source_bottom, column_bottom, 0)
            left_now = lax.dynamic_update_index_in_dim(stores[1], renewed, column_bottom, 1)
            return (entered, left_now, renewed[0])

        def up_spare(stores):
            return (stores[0], stores[1], blank_column)

        live_bottom = (slot_bottom >= 0) & (slot_bottom < local_cols)
        enter_bottom, leave_bottom, send_up = lax.cond(
            live_bottom, up_live, up_spare, (enter_bottom, leave_bottom)
        )
        from_above = shifted(send_down, "rows", 1)
        from_below = shifted(send_up, "rows", -1)
        return (from_above, from_below, enter_top, leave_top, enter_bottom, leave_bottom)

    entry_shape = (local_cols,) + column_shape
    store_shape = (local_rows, local_cols) + column_shape
    initial = (
        blank_column,
        blank_column,
        jnp.zeros(entry_shape, jnp.float32),
        jnp.zeros(store_shape, jnp.float32),
        jnp.zeros(entry_shape, jnp.float32),
        jnp.zeros(store_shape, jnp.float32),
    )
    unused_above, unused_below, enter_top, leave_top, enter_bottom, leave_bottom = lax.fori_loop(
        0, row_count + local_cols - 1, pipe_step, initial
    )
    above = jnp.concatenate([enter_top[None], leave_top[:-1]], axis=0)
    below = jnp.concatenate([leave_bottom[1:], enter_bottom[None]], axis=0)
    global_rows = row_place * local_rows + jnp.arange(local_rows, dtype=jnp.int32)
    global_cols = col_place * local_cols + jnp.arange(local_cols, dtype=jnp.int32)
    row_match = term_rows[:, None] == global_rows[None, :]
    site_match = row_match[:, :, None] & (term_bonds[:, None, None] == global_cols[None, None, :])
    left_need = jnp.any(site_match, axis=0)
    right_need = jnp.any(
        row_match[:, :, None] & (term_bonds[:, None, None] == global_cols[None, None, :] - 1),
        axis=0,
    )
    rows_shape = (local_rows,) + column_shape
    edge_shape = (local_rows, PHYS * PHYS) + column_shape
    open_shape = (local_rows, local_cols, PHYS * PHYS) + column_shape

    def chain_step(section_number, carried):
        from_left, from_right, edge_in, left_opens, right_opens, edge_open = carried

        def left_live(stores):
            source = jnp.where(col_place == 0, left_edge, from_left)
            environ = source[0]
            row_open = []
            for column in range(local_cols):
                opened, environ = side_step(
                    left_core,
                    environ,
                    kets[0, column],
                    layers[0, column],
                    above[0, column],
                    below[0, column],
                    left_need[0, column],
                )
                row_open.append(opened)
            opened_rows = [jnp.stack(row_open)]
            sent_rows = [environ]
            return (jnp.stack(opened_rows), jnp.stack(sent_rows))

        def left_spare(stores):
            return (stores, jnp.zeros(rows_shape, jnp.float32))

        left_opens, sent_left = lax.cond(
            section_number == col_place, left_live, left_spare, left_opens
        )

        def right_live(stores):
            source = jnp.where(col_place == col_count - 1, right_edge, from_right)
            environ = source[0]
            row_open = [None] * local_cols
            for column in reversed(range(local_cols)):
                opened, environ = side_step(
                    right_core,
                    environ,
                    kets[0, column],
                    layers[0, column],
                    above[0, column],
                    below[0, column],
                    right_need[0, column],
                )
                row_open[column] = opened
            opened_rows = [jnp.stack(row_open)]
            sent_rows = [environ]
            kept_edge = stores[1]
            return (jnp.stack(opened_rows), kept_edge, jnp.stack(sent_rows))

        def right_spare(stores):
            return (stores[0], stores[1], jnp.zeros(rows_shape, jnp.float32))

        right_opens, edge_open, sent_right = lax.cond(
            section_number == col_count - 1 - col_place,
            right_live,
            right_spare,
            (right_opens, edge_open),
        )
        from_left = shifted(sent_left, "cols", 1)
        from_right = shifted(sent_right, "cols", -1)
        return (from_left, from_right, edge_in, left_opens, right_opens, edge_open)

    chain_start = (
        jnp.zeros(rows_shape, jnp.float32),
        jnp.zeros(rows_shape, jnp.float32),
        jnp.zeros(edge_shape, jnp.float32),
        jnp.zeros(open_shape, jnp.float32),
        jnp.zeros(open_shape, jnp.float32),
        jnp.zeros(edge_shape, jnp.float32),
    )
    unused_left, unused_right, unused_edge, left_opens, right_opens, edge_open = lax.fori_loop(
        0, col_count, chain_step, chain_start
    )
    edge_open = shifted(right_opens[:, 0], "cols", -1)
    partner = jnp.concatenate([right_opens[:, 1:], edge_open[:, None]], axis=1)
    flat_left = left_opens.reshape(local_rows * local_cols, PHYS * PHYS, -1)
    flat_right = partner.reshape(local_rows * local_cols, PHYS * PHYS, -1)
    density = product("kpz,kqz->kpq", flat_left, flat_right).reshape(local_rows * local_cols, -1)
    diagonal = pair_diagonal()
    weights = jnp.outer(diagonal, diagonal).reshape(-1)
    trace_value = jnp.sum(density * weights[None, :], axis=1)
    spread = jnp.sqrt(jnp.sum(density * density, axis=1))
    valid_bond = left_need.reshape(-1)
    denominator = jnp.where(valid_bond, jnp.maximum(jnp.abs(trace_value), 0.25 * spread), 1.0)
    scaled = density / denominator[:, None]
    chooser = jnp.where(site_match.reshape(TERMS, -1), 1.0, 0.0).astype(jnp.float32)
    chosen = jnp.dot(chooser, scaled, precision=PRECISION_HIGH, preferred_element_type=jnp.float32)
    op_match = jnp.where(
        term_ops[:, None] == jnp.arange(OPS, dtype=jnp.int32)[None, :], 1.0, 0.0
    ).astype(jnp.float32)
    picked = jnp.dot(
        op_match, operators, precision=PRECISION_HIGH, preferred_element_type=jnp.float32
    )
    term_share = jnp.sum(chosen * picked, axis=1)
    energies = lax.psum(term_share, ("rows", "cols"))
    return (leave_top, leave_bottom, energies)


def solution(mesh):
    placed = (
        P("rows", "cols", None),
        P(None, "rows", "cols", None, None),
        P(None, "rows", "cols", None, None),
        P("cols", None, None),
        P("cols", None, None),
        P("rows", None, None),
        P("rows", None, None),
        P(),
        P(),
        P(),
        P(),
    )
    return jax.shard_map(
        shards,
        mesh=mesh,
        in_specs=placed,
        out_specs=(P("rows", "cols", None, None), P("rows", "cols", None, None), P()),
        check_vma=False,
    )
```

profile of v0, /device:TPU:0, one launch (start us, length us, event | category | flops | bytes accessed | tf_op | source)
XLA Modules:
  0.0 565.2 jit_solution(9230488850190270483)
XLA Ops:
  11.3 313.6 %while.90 = (s32[]{:T(128)}, f32[96,384]{1,0:T(8,128)S(1)}, f32[96,384]{1,0:T(8,128)}, f32[2,96,384]{2,1,0:T(8,128)S(1)}, f32[1,2,96,384]{3,2,1,0:T(8,128)}, /*i...) while((s32[]{:T(128)}, f32[96,384]{1,0:T(8,128)S(1)}, ...), condition=%wide.region_7.8_spmd, body=%wide.region_0.7_spmd.sunk | while | flops 736395264 | bytes 20592360 | solution.py:208
  13.3 10.0 %conditional.12 = (f32[2,96,384]{2,1,0:T(8,128)S(1)}, f32[1,2,96,384]{3,2,1,0:T(8,128)}, f32[96,384]{1,0:T(8,128)S(1)}) conditional(s32[]{:T(128)} %convert_element_type.64, (f32[2,96,384]{2,1,0:T(8,128)S(1)}, f32[1,2,96,384]{3,2,1,0:T(8,128)}) %tuple.255, (pred[]{:T(512)}, s32[]{:T(128)}, f32[2,96,384]{2,1,0:T(8,128)}, f32[96,384]{1,0:T(8,128)S(1)}, ...), branch_computations={%region_1.1_spmd, %region_2.3_spmd} | conditional | flops 368197632 | bytes 9593989 | solution.py:172
  27.6 10.0 %conditional.12 = (f32[2,96,384]{2,1,0:T(8,128)S(1)}, f32[1,2,96,384]{3,2,1,0:T(8,128)}, f32[96,384]{1,0:T(8,128)S(1)}) conditional(s32[]{:T(128)} %convert_element_type.64, (f32[2,96,384]{2,1,0:T(8,128)S(1)}, f32[1,2,96,384]{3,2,1,0:T(8,128)}) %tuple.255, (pred[]{:T(512)}, s32[]{:T(128)}, f32[2,96,384]{2,1,0:T(8,128)}, f32[96,384]{1,0:T(8,128)S(1)}, ...), branch_computations={%region_1.1_spmd, %region_2.3_spmd} | conditional | flops 368197632 | bytes 9593989 | solution.py:172
  43.6 13.6 %collective-permute-start = (f32[96,384]{1,0:T(8,128)S(1)}, f32[96,384]{1,0:T(8,128)S(1)}, u32[]{:S(2)}, u32[]{:S(2)}) collective-permute-start(f32[96,384]{1,0:T(8,128)S(1)} %get-tuple-element.1732), channel_id=1, source_target_pairs={{0,2},{2,4},{4,6},{6,8},{8,10},{10,12},{12,14},{14,16},{16,18},{18... | collective-permute-start | bytes 442376 | tf_op jit(solution)/shard_map/while/body/eval_jaxpr/ppermute | solution.py:21
  69.4 16.1 %collective-permute-start = (f32[96,384]{1,0:T(8,128)S(1)}, f32[96,384]{1,0:T(8,128)S(1)}, u32[]{:S(2)}, u32[]{:S(2)}) collective-permute-start(f32[96,384]{1,0:T(8,128)S(1)} %get-tuple-element.1732), channel_id=1, source_target_pairs={{0,2},{2,4},{4,6},{6,8},{8,10},{10,12},{12,14},{14,16},{16,18},{18... | collective-permute-start | bytes 442376 | tf_op jit(solution)/shard_map/while/body/eval_jaxpr/ppermute | solution.py:21
  97.5 13.0 %collective-permute-start = (f32[96,384]{1,0:T(8,128)S(1)}, f32[96,384]{1,0:T(8,128)S(1)}, u32[]{:S(2)}, u32[]{:S(2)}) collective-permute-start(f32[96,384]{1,0:T(8,128)S(1)} %get-tuple-element.1732), channel_id=1, source_target_pairs={{0,2},{2,4},{4,6},{6,8},{8,10},{10,12},{12,14},{14,16},{16,18},{18... | collective-permute-start | bytes 442376 | tf_op jit(solution)/shard_map/while/body/eval_jaxpr/ppermute | solution.py:21
  122.7 15.4 %collective-permute-start = (f32[96,384]{1,0:T(8,128)S(1)}, f32[96,384]{1,0:T(8,128)S(1)}, u32[]{:S(2)}, u32[]{:S(2)}) collective-permute-start(f32[96,384]{1,0:T(8,128)S(1)} %get-tuple-element.1732), channel_id=1, source_target_pairs={{0,2},{2,4},{4,6},{6,8},{8,10},{10,12},{12,14},{14,16},{16,18},{18... | collective-permute-start | bytes 442376 | tf_op jit(solution)/shard_map/while/body/eval_jaxpr/ppermute | solution.py:21
  141.1 8.6 %collective-permute-start = (f32[96,384]{1,0:T(8,128)S(1)}, f32[96,384]{1,0:T(8,128)S(1)}, u32[]{:S(2)}, u32[]{:S(2)}) collective-permute-start(f32[96,384]{1,0:T(8,128)S(1)} %get-tuple-element.1732), channel_id=1, source_target_pairs={{0,2},{2,4},{4,6},{6,8},{8,10},{10,12},{12,14},{14,16},{16,18},{18... | collective-permute-start | bytes 442376 | tf_op jit(solution)/shard_map/while/body/eval_jaxpr/ppermute | solution.py:21
  152.7 11.5 %collective-permute-start = (f32[96,384]{1,0:T(8,128)S(1)}, f32[96,384]{1,0:T(8,128)S(1)}, u32[]{:S(2)}, u32[]{:S(2)}) collective-permute-start(f32[96,384]{1,0:T(8,128)S(1)} %get-tuple-element.1732), channel_id=1, source_target_pairs={{0,2},{2,4},{4,6},{6,8},{8,10},{10,12},{12,14},{14,16},{16,18},{18... | collective-permute-start | bytes 442376 | tf_op jit(solution)/shard_map/while/body/eval_jaxpr/ppermute | solution.py:21
  167.1 8.6 %collective-permute-start = (f32[96,384]{1,0:T(8,128)S(1)}, f32[96,384]{1,0:T(8,128)S(1)}, u32[]{:S(2)}, u32[]{:S(2)}) collective-permute-start(f32[96,384]{1,0:T(8,128)S(1)} %get-tuple-element.1732), channel_id=1, source_target_pairs={{0,2},{2,4},{4,6},{6,8},{8,10},{10,12},{12,14},{14,16},{16,18},{18... | collective-permute-start | bytes 442376 | tf_op jit(solution)/shard_map/while/body/eval_jaxpr/ppermute | solution.py:21
  178.8 11.1 %collective-permute-start = (f32[96,384]{1,0:T(8,128)S(1)}, f32[96,384]{1,0:T(8,128)S(1)}, u32[]{:S(2)}, u32[]{:S(2)}) collective-permute-start(f32[96,384]{1,0:T(8,128)S(1)} %get-tuple-element.1732), channel_id=1, source_target_pairs={{0,2},{2,4},{4,6},{6,8},{8,10},{10,12},{12,14},{14,16},{16,18},{18... | collective-permute-start | bytes 442376 | tf_op jit(solution)/shard_map/while/body/eval_jaxpr/ppermute | solution.py:21
  202.8 83.8 %collective-permute-start = (f32[96,384]{1,0:T(8,128)S(1)}, f32[96,384]{1,0:T(8,128)S(1)}, u32[]{:S(2)}, u32[]{:S(2)}) collective-permute-start(f32[96,384]{1,0:T(8,128)S(1)} %get-tuple-element.1732), channel_id=1, source_target_pairs={{0,2},{2,4},{4,6},{6,8},{8,10},{10,12},{12,14},{14,16},{16,18},{18... | collective-permute-start | bytes 442376 | tf_op jit(solution)/shard_map/while/body/eval_jaxpr/ppermute | solution.py:21
  287.7 11.3 %conditional.13 = (f32[2,96,384]{2,1,0:T(8,128)S(1)}, f32[1,2,96,384]{3,2,1,0:T(8,128)}, f32[96,384]{1,0:T(8,128)}) conditional(s32[]{:T(128)} %convert_element_type.65, (f32[2,96,384]{2,1,0:T(8,128)S(1)}, f32[1,2,96,384]{3,2,1,0:T(8,128)}) %tuple.257, (pred[]{:T(512)}, s32[]{:T(128)}, f32[2,96,384]{2,1,0:T(8,128)}, f32[96,384]{1,0:T(8,128)}, ...), branch_computations={%region_4.4_spmd, %region_5.6_spmd} | conditional | flops 368197632 | bytes 9818217 | solution.py:191
  308.3 11.3 %conditional.13 = (f32[2,96,384]{2,1,0:T(8,128)S(1)}, f32[1,2,96,384]{3,2,1,0:T(8,128)}, f32[96,384]{1,0:T(8,128)}) conditional(s32[]{:T(128)} %convert_element_type.65, (f32[2,96,384]{2,1,0:T(8,128)S(1)}, f32[1,2,96,384]{3,2,1,0:T(8,128)}) %tuple.257, (pred[]{:T(512)}, s32[]{:T(128)}, f32[2,96,384]{2,1,0:T(8,128)}, f32[96,384]{1,0:T(8,128)}, ...), branch_computations={%region_4.4_spmd, %region_5.6_spmd} | conditional | flops 368197632 | bytes 9818217 | solution.py:191
  327.3 126.6 %while.91 = (s32[]{:T(128)}, f32[1,96,384]{2,1,0:T(8,128)S(1)}, f32[1,96,384]{2,1,0:T(8,128)S(1)}, f32[1,2,4,96,384]{4,3,2,1,0:T(8,128)}, f32[1,2,4,96,384]{4,3,...) while((s32[]{:T(128)}, f32[1,96,384]{2,1,0:T(8,128)S(1)}, ...), condition=%wide.region_43.44_spmd, body=%wide.region_10.43_spmd.sunk | while | flops 1474342912 | bytes 33713392 | solution.py:296
  327.6 38.6 %conditional.14 = (f32[1,2,4,96,384]{4,3,2,1,0:T(8,128)}, f32[1,96,384]{2,1,0:T(8,128)}) conditional(s32[]{:T(128)} %convert_element_type.66, f32[1,2,4,96,384]{4,3,2,1,0:T(8,128)} %get-tuple-element.1977, (pred[1,2]{1,0:T(4,128)(4,1)S(1)}, s32[]{:T(128)}, f32[1,96,384]{1,2,0:T(8,128)S(1)}, f32[1,96,384]{2,1,0:T(8,128)S(1)}, ...), branch_computations={%region_11.11_spmd, %region_12.26_spmd} | conditional | flops 737171456 | bytes 16268730 | solution.py:251
  329.1 25.6 %conditional.2 = (f32[96,384]{1,0:T(8,128)S(1)}, f32[1,4,96,384]{3,2,1,0:T(8,128)}) conditional(s32[]{:T(128)} %bitcast.85, (f32[1,96,384]{1,2,0:T(8,128)S(1)}, f32[1,1,96,384]{3,2,1,0:T(8,128)S(1)}, f32[1,2,4,4,4,4]{2,5,3,4,1,0:T(4,128)S(1)}, f32[1,1,96,384]{3,2,1,0:T(8,128)S(1)}) %tuple.128, (f32[1,2,32]{2,1,0:T(2,128)S(1)}, ...), branch_computations={%region_13.13_spmd, %region_15.18_spmd} | conditional | flops 368419840 | bytes 5846665 | solution.py:106
  329.8 22.3 %while.86 = (s32[]{:T(128)}, f32[4,96,384]{2,1,0:T(8,128)}, f32[1,96,384]{1,2,0:T(8,128)S(1)}, f32[1,1,96,384]{3,2,1,0:T(8,128)S(1)}, f32[4,4,4,4,4]{1,4,2,3,0:T...) while((s32[]{:T(128)}, f32[4,96,384]{2,1,0:T(8,128)}, f32[1,96,384]{1,2,0:T(8,128)S(1)}, ...), condition=%wide.region_17.15_spmd, body=%wide.region_16.14_spmd.sunk | while | flops 368050176 | bytes 4653649 | solution.py:96
  381.8 14.2 %conditional.14 = (f32[1,2,4,96,384]{4,3,2,1,0:T(8,128)}, f32[1,96,384]{2,1,0:T(8,128)}) conditional(s32[]{:T(128)} %convert_element_type.66, f32[1,2,4,96,384]{4,3,2,1,0:T(8,128)} %get-tuple-element.1977, (pred[1,2]{1,0:T(4,128)(4,1)S(1)}, s32[]{:T(128)}, f32[1,96,384]{1,2,0:T(8,128)S(1)}, f32[1,96,384]{2,1,0:T(8,128)S(1)}, ...), branch_computations={%region_11.11_spmd, %region_12.26_spmd} | conditional | flops 737171456 | bytes 16268730 | solution.py:251
  403.5 38.4 %conditional.15 = (f32[1,2,4,96,384]{4,3,2,1,0:T(8,128)}, f32[1,96,384]{2,1,0:T(8,128)}) conditional(s32[]{:T(128)} %convert_element_type.67, f32[1,2,4,96,384]{4,3,2,1,0:T(8,128)} %get-tuple-element.1978, (pred[1,2]{1,0:T(4,128)(4,1)S(1)}, s32[]{:T(128)}, f32[1,96,384]{1,2,0:T(8,128)S(1)}, f32[1,96,384]{2,1,0:T(8,128)S(1)}, ...), branch_computations={%region_27.27_spmd, %region_28.42_spmd} | conditional | flops 737171456 | bytes 16264634 | solution.py:278
  405.0 25.5 %conditional.4 = (f32[96,384]{1,0:T(8,128)S(1)}, f32[1,4,96,384]{3,2,1,0:T(8,128)}) conditional(s32[]{:T(128)} %bitcast.142, (f32[1,96,384]{1,2,0:T(8,128)S(1)}, f32[1,1,96,384]{3,2,1,0:T(8,128)S(1)}, f32[1,2,4,4,4,4]{2,4,5,3,1,0:T(4,128)S(1)}, f32[1,1,96,384]{3,2,1,0:T(8,128)S(1)}) %tuple.142, (f32[1,2,32]{2,1,0:T(2,128)S(1)}, ...), branch_computations={%region_29.29_spmd, %region_31.34_spmd} | conditional | flops 368419840 | bytes 5846665 | solution.py:106
  405.6 22.3 %while.88 = (s32[]{:T(128)}, f32[4,96,384]{2,1,0:T(8,128)}, f32[1,96,384]{1,2,0:T(8,128)S(1)}, f32[1,1,96,384]{3,2,1,0:T(8,128)S(1)}, f32[4,4,4,4,4]{1,3,4,2,0:T...) while((s32[]{:T(128)}, f32[4,96,384]{2,1,0:T(8,128)}, f32[1,96,384]{1,2,0:T(8,128)S(1)}, ...), condition=%wide.region_33.31_spmd, body=%wide.region_32.30_spmd.sunk | while | flops 368050176 | bytes 4653649 | solution.py:96
  459.5 8.4 %collective-permute-done.4 = f32[1,4,96,384]{3,2,1,0:T(8,128)S(1)} collective-permute-done((f32[1,4,96,384]{3,2,1,0:T(8,128)}, f32[1,4,96,384]{3,2,1,0:T(8,128)S(1)}, u32[]{:S(2)}, u32[]{:S(2)}) %collective-permute-start.4) | collective-permute-done | bytes 589856 | tf_op jit(solution)/shard_map/ppermute | solution.py:21
  474.9 89.8 %psum.7 = f32[16]{0:T(128)} all-reduce(f32[16]{0:T(128)S(1)} %fusion.86), channel_id=1, replica_groups=mesh['rows'=16,'cols'=2] {'rows','cols'}, use_global_device_ids=true, to_apply=%region_47.48 | all-reduce | flops 16 | bytes 128 | tf_op jit(solution)/shard_map/psum | solution.py:320
  (375 shorter events, 281.2 us)
Async XLA Ops:
  12.0 12.6 %collective-permute-start.1 = (f32[96,384]{1,0:T(8,128)}, f32[96,384]{1,0:T(8,128)}, u32[]{:S(2)}, u32[]{:S(2)}) collective-permute-start(f32[96,384]{1,0:T(8,128)} %get-tuple-element.1733), channel_id=1, source_target_pairs={{2,0},{4,2},{6,4},{8,6},{10,8},{12,10},{14,12},{16,14},{18,16},{20... | collective-permute-start | bytes 442376 | tf_op jit(solution)/shard_map/while/body/eval_jaxpr/ppermute | solution.py:21
  26.3 14.4 %collective-permute-start.1 = (f32[96,384]{1,0:T(8,128)}, f32[96,384]{1,0:T(8,128)}, u32[]{:S(2)}, u32[]{:S(2)}) collective-permute-start(f32[96,384]{1,0:T(8,128)} %get-tuple-element.1733), channel_id=1, source_target_pairs={{2,0},{4,2},{6,4},{8,6},{10,8},{12,10},{14,12},{16,14},{18,16},{20... | collective-permute-start | bytes 442376 | tf_op jit(solution)/shard_map/while/body/eval_jaxpr/ppermute | solution.py:21
  42.3 15.0 %collective-permute-start.1 = (f32[96,384]{1,0:T(8,128)}, f32[96,384]{1,0:T(8,128)}, u32[]{:S(2)}, u32[]{:S(2)}) collective-permute-start(f32[96,384]{1,0:T(8,128)} %get-tuple-element.1733), channel_id=1, source_target_pairs={{2,0},{4,2},{6,4},{8,6},{10,8},{12,10},{14,12},{16,14},{18,16},{20... | collective-permute-start | bytes 442376 | tf_op jit(solution)/shard_map/while/body/eval_jaxpr/ppermute | solution.py:21
  43.6 14.6 %collective-permute-start = (f32[96,384]{1,0:T(8,128)S(1)}, f32[96,384]{1,0:T(8,128)S(1)}, u32[]{:S(2)}, u32[]{:S(2)}) collective-permute-start(f32[96,384]{1,0:T(8,128)S(1)} %get-tuple-element.1732), channel_id=1, source_target_pairs={{0,2},{2,4},{4,6},{6,8},{8,10},{10,12},{12,14},{14,16},{16,18},{18... | collective-permute-start | bytes 442376 | tf_op jit(solution)/shard_map/while/body/eval_jaxpr/ppermute | solution.py:21
  68.0 17.4 %collective-permute-start.1 = (f32[96,384]{1,0:T(8,128)}, f32[96,384]{1,0:T(8,128)}, u32[]{:S(2)}, u32[]{:S(2)}) collective-permute-start(f32[96,384]{1,0:T(8,128)} %get-tuple-element.1733), channel_id=1, source_target_pairs={{2,0},{4,2},{6,4},{8,6},{10,8},{12,10},{14,12},{16,14},{18,16},{20... | collective-permute-start | bytes 442376 | tf_op jit(solution)/shard_map/while/body/eval_jaxpr/ppermute | solution.py:21
  69.4 17.1 %collective-permute-start = (f32[96,384]{1,0:T(8,128)S(1)}, f32[96,384]{1,0:T(8,128)S(1)}, u32[]{:S(2)}, u32[]{:S(2)}) collective-permute-start(f32[96,384]{1,0:T(8,128)S(1)} %get-tuple-element.1732), channel_id=1, source_target_pairs={{0,2},{2,4},{4,6},{6,8},{8,10},{10,12},{12,14},{14,16},{16,18},{18... | collective-permute-start | bytes 442376 | tf_op jit(solution)/shard_map/while/body/eval_jaxpr/ppermute | solution.py:21
  96.2 14.4 %collective-permute-start.1 = (f32[96,384]{1,0:T(8,128)}, f32[96,384]{1,0:T(8,128)}, u32[]{:S(2)}, u32[]{:S(2)}) collective-permute-start(f32[96,384]{1,0:T(8,128)} %get-tuple-element.1733), channel_id=1, source_target_pairs={{2,0},{4,2},{6,4},{8,6},{10,8},{12,10},{14,12},{16,14},{18,16},{20... | collective-permute-start | bytes 442376 | tf_op jit(solution)/shard_map/while/body/eval_jaxpr/ppermute | solution.py:21
  97.5 14.0 %collective-permute-start = (f32[96,384]{1,0:T(8,128)S(1)}, f32[96,384]{1,0:T(8,128)S(1)}, u32[]{:S(2)}, u32[]{:S(2)}) collective-permute-start(f32[96,384]{1,0:T(8,128)S(1)} %get-tuple-element.1732), channel_id=1, source_target_pairs={{0,2},{2,4},{4,6},{6,8},{8,10},{10,12},{12,14},{14,16},{16,18},{18... | collective-permute-start | bytes 442376 | tf_op jit(solution)/shard_map/while/body/eval_jaxpr/ppermute | solution.py:21
  121.3 16.8 %collective-permute-start.1 = (f32[96,384]{1,0:T(8,128)}, f32[96,384]{1,0:T(8,128)}, u32[]{:S(2)}, u32[]{:S(2)}) collective-permute-start(f32[96,384]{1,0:T(8,128)} %get-tuple-element.1733), channel_id=1, source_target_pairs={{2,0},{4,2},{6,4},{8,6},{10,8},{12,10},{14,12},{16,14},{18,16},{20... | collective-permute-start | bytes 442376 | tf_op jit(solution)/shard_map/while/body/eval_jaxpr/ppermute | solution.py:21
  122.7 16.4 %collective-permute-start = (f32[96,384]{1,0:T(8,128)S(1)}, f32[96,384]{1,0:T(8,128)S(1)}, u32[]{:S(2)}, u32[]{:S(2)}) collective-permute-start(f32[96,384]{1,0:T(8,128)S(1)} %get-tuple-element.1732), channel_id=1, source_target_pairs={{0,2},{2,4},{4,6},{6,8},{8,10},{10,12},{12,14},{14,16},{16,18},{18... | collective-permute-start | bytes 442376 | tf_op jit(solution)/shard_map/while/body/eval_jaxpr/ppermute | solution.py:21
  139.7 9.9 %collective-permute-start.1 = (f32[96,384]{1,0:T(8,128)}, f32[96,384]{1,0:T(8,128)}, u32[]{:S(2)}, u32[]{:S(2)}) collective-permute-start(f32[96,384]{1,0:T(8,128)} %get-tuple-element.1733), channel_id=1, source_target_pairs={{2,0},{4,2},{6,4},{8,6},{10,8},{12,10},{14,12},{16,14},{18,16},{20... | collective-permute-start | bytes 442376 | tf_op jit(solution)/shard_map/while/body/eval_jaxpr/ppermute | solution.py:21
  141.1 9.6 %collective-permute-start = (f32[96,384]{1,0:T(8,128)S(1)}, f32[96,384]{1,0:T(8,128)S(1)}, u32[]{:S(2)}, u32[]{:S(2)}) collective-permute-start(f32[96,384]{1,0:T(8,128)S(1)} %get-tuple-element.1732), channel_id=1, source_target_pairs={{0,2},{2,4},{4,6},{6,8},{8,10},{10,12},{12,14},{14,16},{16,18},{18... | collective-permute-start | bytes 442376 | tf_op jit(solution)/shard_map/while/body/eval_jaxpr/ppermute | solution.py:21
  151.3 12.8 %collective-permute-start.1 = (f32[96,384]{1,0:T(8,128)}, f32[96,384]{1,0:T(8,128)}, u32[]{:S(2)}, u32[]{:S(2)}) collective-permute-start(f32[96,384]{1,0:T(8,128)} %get-tuple-element.1733), channel_id=1, source_target_pairs={{2,0},{4,2},{6,4},{8,6},{10,8},{12,10},{14,12},{16,14},{18,16},{20... | collective-permute-start | bytes 442376 | tf_op jit(solution)/shard_map/while/body/eval_jaxpr/ppermute | solution.py:21
  152.7 12.5 %collective-permute-start = (f32[96,384]{1,0:T(8,128)S(1)}, f32[96,384]{1,0:T(8,128)S(1)}, u32[]{:S(2)}, u32[]{:S(2)}) collective-permute-start(f32[96,384]{1,0:T(8,128)S(1)} %get-tuple-element.1732), channel_id=1, source_target_pairs={{0,2},{2,4},{4,6},{6,8},{8,10},{10,12},{12,14},{14,16},{16,18},{18... | collective-permute-start | bytes 442376 | tf_op jit(solution)/shard_map/while/body/eval_jaxpr/ppermute | solution.py:21
  165.8 10.0 %collective-permute-start.1 = (f32[96,384]{1,0:T(8,128)}, f32[96,384]{1,0:T(8,128)}, u32[]{:S(2)}, u32[]{:S(2)}) collective-permute-start(f32[96,384]{1,0:T(8,128)} %get-tuple-element.1733), channel_id=1, source_target_pairs={{2,0},{4,2},{6,4},{8,6},{10,8},{12,10},{14,12},{16,14},{18,16},{20... | collective-permute-start | bytes 442376 | tf_op jit(solution)/shard_map/while/body/eval_jaxpr/ppermute | solution.py:21
  167.1 9.6 %collective-permute-start = (f32[96,384]{1,0:T(8,128)S(1)}, f32[96,384]{1,0:T(8,128)S(1)}, u32[]{:S(2)}, u32[]{:S(2)}) collective-permute-start(f32[96,384]{1,0:T(8,128)S(1)} %get-tuple-element.1732), channel_id=1, source_target_pairs={{0,2},{2,4},{4,6},{6,8},{8,10},{10,12},{12,14},{14,16},{16,18},{18... | collective-permute-start | bytes 442376 | tf_op jit(solution)/shard_map/while/body/eval_jaxpr/ppermute | solution.py:21
  177.4 12.4 %collective-permute-start.1 = (f32[96,384]{1,0:T(8,128)}, f32[96,384]{1,0:T(8,128)}, u32[]{:S(2)}, u32[]{:S(2)}) collective-permute-start(f32[96,384]{1,0:T(8,128)} %get-tuple-element.1733), channel_id=1, source_target_pairs={{2,0},{4,2},{6,4},{8,6},{10,8},{12,10},{14,12},{16,14},{18,16},{20... | collective-permute-start | bytes 442376 | tf_op jit(solution)/shard_map/while/body/eval_jaxpr/ppermute | solution.py:21
  178.8 12.0 %collective-permute-start = (f32[96,384]{1,0:T(8,128)S(1)}, f32[96,384]{1,0:T(8,128)S(1)}, u32[]{:S(2)}, u32[]{:S(2)}) collective-permute-start(f32[96,384]{1,0:T(8,128)S(1)} %get-tuple-element.1732), channel_id=1, source_target_pairs={{0,2},{2,4},{4,6},{6,8},{8,10},{10,12},{12,14},{14,16},{16,18},{18... | collective-permute-start | bytes 442376 | tf_op jit(solution)/shard_map/while/body/eval_jaxpr/ppermute | solution.py:21
  201.5 85.2 %collective-permute-start.1 = (f32[96,384]{1,0:T(8,128)}, f32[96,384]{1,0:T(8,128)}, u32[]{:S(2)}, u32[]{:S(2)}) collective-permute-start(f32[96,384]{1,0:T(8,128)} %get-tuple-element.1733), channel_id=1, source_target_pairs={{2,0},{4,2},{6,4},{8,6},{10,8},{12,10},{14,12},{16,14},{18,16},{20... | collective-permute-start | bytes 442376 | tf_op jit(solution)/shard_map/while/body/eval_jaxpr/ppermute | solution.py:21
  202.8 84.8 %collective-permute-start = (f32[96,384]{1,0:T(8,128)S(1)}, f32[96,384]{1,0:T(8,128)S(1)}, u32[]{:S(2)}, u32[]{:S(2)}) collective-permute-start(f32[96,384]{1,0:T(8,128)S(1)} %get-tuple-element.1732), channel_id=1, source_target_pairs={{0,2},{2,4},{4,6},{6,8},{8,10},{10,12},{12,14},{14,16},{16,18},{18... | collective-permute-start | bytes 442376 | tf_op jit(solution)/shard_map/while/body/eval_jaxpr/ppermute | solution.py:21
  298.9 8.4 %collective-permute-start.1 = (f32[96,384]{1,0:T(8,128)}, f32[96,384]{1,0:T(8,128)}, u32[]{:S(2)}, u32[]{:S(2)}) collective-permute-start(f32[96,384]{1,0:T(8,128)} %get-tuple-element.1733), channel_id=1, source_target_pairs={{2,0},{4,2},{6,4},{8,6},{10,8},{12,10},{14,12},{16,14},{18,16},{20... | collective-permute-start | bytes 442376 | tf_op jit(solution)/shard_map/while/body/eval_jaxpr/ppermute | solution.py:21
  366.2 9.4 %collective-permute-start.2 = (f32[1,96,384]{2,1,0:T(8,128)}, f32[1,96,384]{2,1,0:T(8,128)S(1)}, u32[]{:S(2)}, u32[]{:S(2)}) collective-permute-start(f32[1,96,384]{2,1,0:T(8,128)} %get-tuple-element.1753), channel_id=1, source_target_pairs={{0,1},{2,3},{4,5},{6,7},{8,9},{10,11},{12,13},{14,15},{16,17},{18,... | collective-permute-start | bytes 442376 | tf_op jit(solution)/shard_map/while/body/eval_jaxpr/ppermute | solution.py:21
  396.0 47.3 %collective-permute-start.2 = (f32[1,96,384]{2,1,0:T(8,128)}, f32[1,96,384]{2,1,0:T(8,128)S(1)}, u32[]{:S(2)}, u32[]{:S(2)}) collective-permute-start(f32[1,96,384]{2,1,0:T(8,128)} %get-tuple-element.1753), channel_id=1, source_target_pairs={{0,1},{2,3},{4,5},{6,7},{8,9},{10,11},{12,13},{14,15},{16,17},{18,... | collective-permute-start | bytes 442376 | tf_op jit(solution)/shard_map/while/body/eval_jaxpr/ppermute | solution.py:21
  456.0 12.0 %collective-permute-start.4 = (f32[1,4,96,384]{3,2,1,0:T(8,128)}, f32[1,4,96,384]{3,2,1,0:T(8,128)S(1)}, u32[]{:S(2)}, u32[]{:S(2)}) collective-permute-start(f32[1,4,96,384]{3,2,1,0:T(8,128)} %get-tuple-element.1421), channel_id=1, source_target_pairs={{1,0},{3,2},{5,4},{7,6},{9,8},{11,10},{13,12},{15,14},{17,16},{19,... | collective-permute-start | bytes 1769480 | tf_op jit(solution)/shard_map/ppermute | solution.py:21
  (33 other events, 634.3 us)
where the time goes:
time: 565 us
  starting transfers between devices  256 us (45%)
  blocking collectives  89.8 us (16%)
  matrix products  74.9 us (13%)
  local copies, waits for them, and re-layouts  55.9 us (10%)
  waiting for transfers between devices  36.8 us (7%)
  loops' own time  36.3 us (6%)
  other arithmetic  14.2 us (3%)
    ppermute x39, starting transfers between devices, shifted(): lax.ppermute(value, axis, [(source, source + steps) for source in range(i...  256 us
    psum x1, blocking collectives, shards(): energies = lax.psum(term_share, ('rows', 'cols'))  89.8 us
    dot_general x44, matrix products, product(): jnp.einsum(pattern, former, latter, precision=PRECISION_HIGH, preferred_e...  74.5 us
    ppermute x39, waiting for transfers between devices, shifted(): lax.ppermute(value, axis, [(source, source + steps) for source in range(i...  36.8 us
    another operation x2, loops' own time, chain_step(): lax.cond(section_number == col_place, left_live, left_spare, left_opens)  15.3 us
  transfers between devices with their start and end apart: 39, of which 20 were waited for; matrix products, arithmetic and copies ran while one was open for 10% of the time, Pallas kernels for 0%

commit v1 on v0

--- a/solution.py
+++ b/solution.py
@@ -1,6 +1,10 @@
+import functools
+
 import jax
 import jax.numpy as jnp
 from jax import lax
+from jax.experimental import pallas as pl
+from jax.experimental.pallas import tpu as pltpu
 from jax.sharding import PartitionSpec as P
 
 D = 2
@@ -12,7 +16,7 @@
 
 
 EPSILON = 1e-06
-PRECISION_HIGH = lax.Precision.HIGHEST
+PRECISION_HIGH = lax.Precision.HIGH
 
 
 def shifted(value, axis, steps):
@@ -50,26 +54,6 @@
 def pair_diagonal():
     matched = jnp.arange(PHYS)[:, None] == jnp.arange(PHYS)[None, :]
     return jnp.where(matched, 1.0, 0.0).astype(jnp.float32).reshape(PHYS * PHYS)
-
-
-def absorb_down(boundary, layers, left_map, right_map):
-    above_col = boundary.reshape(CHI, D2, CHI)
-    left_three = left_map.reshape(CHI, CHI, D2)
-    right_three = right_map.reshape(CHI, CHI, D2)
-    joined = product("aub,cbr->aurc", above_col, right_three)
-    through = product("aurc,uldr->aldc", joined, layers)
-    renewed = product("xal,aldc->xdc", left_three, through)
-    return normalize(renewed.reshape(CHI, D2 * CHI))
-
-
-def absorb_up(boundary, layers, left_map, right_map):
-    below_col = boundary.reshape(CHI, D2, CHI)
-    left_three = left_map.reshape(CHI, CHI, D2)
-    right_three = right_map.reshape(CHI, CHI, D2)
-    joined = product("adb,cbr->adrc", below_col, right_three)
-    through = product("adrc,uldr->aluc", joined, layers)
-    renewed = product("xal,aluc->xuc", left_three, through)
-    return normalize(renewed.reshape(CHI, D2 * CHI))
 
 
 def left_core(environ, layers, above_col, below_col):
@@ -104,6 +88,400 @@
         return (empty_open, normalize(core_map(environ, layers, above_col, below_col)))
 
     return lax.cond(wanted, with_open, without_open, 0)
+
+
+LANES = 128
+
+
+def unpack_lanes(tiles, chi):
+    rolled = {}
+    lane = lax.broadcasted_iota(jnp.int32, tiles[0].shape, 1)
+    blocks = []
+    for block in range(D2):
+        total = jnp.zeros_like(tiles[0])
+        for place, tile in enumerate(tiles):
+            low = max(chi * block, LANES * place)
+            high = min(chi * (block + 1), LANES * (place + 1))
+            if low >= high:
+                continue
+            shift = (LANES * place - chi * block) % LANES
+            if (place, shift) not in rolled:
+                rolled[place, shift] = tile if shift == 0 else pltpu.roll(tile, shift, 1)
+            inside = (lane >= low - chi * block) & (lane < high - chi * block)
+            total = jnp.where(inside, rolled[place, shift], total)
+        blocks.append(total)
+    return blocks
+
+
+def pack_lanes(blocks, chi):
+    lane = lax.broadcasted_iota(jnp.int32, blocks[0].shape, 1)
+    rolled = {}
+    tiles = []
+    for place in range(chi * D2 // LANES):
+        total = jnp.zeros_like(blocks[0])
+        for block, values in enumerate(blocks):
+            low = max(chi * block, LANES * place)
+            high = min(chi * (block + 1), LANES * (place + 1))
+            if low >= high:
+                continue
+            shift = (chi * block - LANES * place) % LANES
+            if (block, shift) not in rolled:
+                rolled[block, shift] = values if shift == 0 else pltpu.roll(values, shift, 1)
+            inside = (lane >= low - LANES * place) & (lane < high - LANES * place)
+            total = jnp.where(inside, rolled[block, shift], total)
+        tiles.append(total)
+    return tiles
+
+
+def halves(values):
+    high = values.astype(jnp.bfloat16)
+    low = (values - high.astype(jnp.float32)).astype(jnp.bfloat16)
+    return high, low
+
+
+def dot32(former, latter):
+    return jnp.dot(former, latter, preferred_element_type=jnp.float32)
+
+
+def dot_last(former, latter):
+    return lax.dot_general(
+        former, latter, (((1,), (1,)), ((), ())), preferred_element_type=jnp.float32
+    )
+
+
+def load_tiles(ref, at, width):
+    return [ref[at, :, LANES * t : LANES * (t + 1)] for t in range(width // LANES)]
+
+
+def chain_kernel(
+    row_count,
+    kets_ref,
+    left_ref,
+    right_ref,
+    top_ref,
+    bottom_ref,
+    out_ref,
+    env_ref,
+    pbuf,
+    qbuf,
+    kbuf,
+    xbuf,
+    ebuf,
+    pick,
+    phi,
+    plo,
+    qhi,
+    qlo,
+    x32,
+    jbuf,
+    thi,
+    tlo,
+    map_send,
+    map_recv,
+    env_send,
+    env_recv,
+    out_send,
+    out_recv,
+    hop_send,
+    hop_recv,
+):
+    local_cols = kets_ref.shape[1]
+    chi, width = left_ref.shape[2], left_ref.shape[3]
+    group = 2 * local_cols
+    groups = row_count // group
+    place = lax.axis_index("rows")
+    mine = place // group
+    me = place % group
+    column = me // 2
+    way = me % 2
+    base = mine * group
+    before = mine - 1 + 2 * way
+    after = mine + 1 - 2 * way
+    has_before = (before >= 0) & (before < groups)
+    has_after = (after >= 0) & (after < groups)
+
+    barrier = pltpu.get_barrier_semaphore()
+    for other in range(group):
+
+        @pl.when(me != other)
+        def _():
+            pl.semaphore_signal(barrier, inc=1, device_id={"rows": base + other})
+
+    @pl.when(has_before)
+    def _():
+        pl.semaphore_signal(barrier, inc=1, device_id={"rows": before * group + me})
+
+    @pl.when(has_after)
+    def _():
+        pl.semaphore_signal(barrier, inc=1, device_id={"rows": after * group + me})
+
+    waits = group - 1 + jnp.where(has_before, 1, 0) + jnp.where(has_after, 1, 0)
+    pl.semaphore_wait(barrier, waits)
+
+    def map_copies(target_way, target_col, target, local):
+        made = []
+        for kind, (source, buffer) in enumerate(
+            ((kets_ref, kbuf), (right_ref, qbuf), (left_ref, pbuf))
+        ):
+            origin, landing = source.at[target_way, target_col], buffer.at[me]
+            if local:
+                made.append(pltpu.make_async_copy(origin, landing, map_recv.at[kind, me]))
+            else:
+                made.append(
+                    pltpu.make_async_remote_copy(
+                        origin,
+                        landing,
+                        map_send.at[kind, target],
+                        map_recv.at[kind, me],
+                        device_id={"rows": base + target},
+                    )
+                )
+        return made
+
+    late = jnp.where(mine >= groups // 2, 1, 0)
+    for turn in range(group):
+        target_way = (late + turn // local_cols) % 2
+        target_col = turn % local_cols
+        target = target_col * 2 + target_way
+
+        @pl.when(target != me)
+        def _():
+            for copy in map_copies(target_way, target_col, target, False):
+                copy.start()
+
+        @pl.when(target == me)
+        def _():
+            for copy in map_copies(target_way, target_col, target, True):
+                copy.start()
+
+    chosen = lax.broadcasted_iota(jnp.int32, (D2 * LANES, width), 0)
+    entry = lax.broadcasted_iota(jnp.int32, (D2 * LANES, width), 1)
+    wanted = (chosen % LANES) * D2 + chosen // LANES
+    live = (chosen % LANES) < chi
+    pick[...] = jnp.where((wanted == entry) & live, 1.0, 0.0).astype(jnp.bfloat16)
+    thi[...] = jnp.zeros_like(thi)
+    tlo[...] = jnp.zeros_like(tlo)
+
+    def prepare(step, unused):
+        slot = step + way * (group - 1 - 2 * step)
+        for kind, buffer in enumerate((kbuf, qbuf, pbuf)):
+            pltpu.make_async_copy(
+                buffer.at[slot], buffer.at[slot], map_recv.at[kind, slot]
+            ).wait()
+        ket = kbuf[slot]
+        half = ket.shape[0] // PHYS
+        for i in range(half):
+            total = ket[i : i + 1] * ket[0:half]
+            for p in range(1, PHYS):
+                total += ket[p * half + i : p * half + i + 1] * ket[p * half : (p + 1) * half]
+            ebuf[step, i * half : (i + 1) * half] = total
+        values = pick[...]
+        for source, high_ref, low_ref, right in (
+            (qbuf, qhi, qlo, True),
+            (pbuf, phi, plo, False),
+        ):
+            for part, ref in zip(halves(source[slot]), (high_ref, low_ref)):
+                if right:
+                    fill = jnp.zeros((LANES - chi, width), jnp.bfloat16)
+                    tall = dot_last(values, jnp.concatenate([part, fill], axis=0))
+                    for w in range(D2):
+                        ref[step, :, w * LANES : (w + 1) * LANES] = tall[
+                            w * LANES : (w + 1) * LANES
+                        ].astype(jnp.bfloat16)
+                else:
+                    ref[step] = dot_last(part, values).astype(jnp.bfloat16)
+        return unused
+
+    def row_copy(source, landing, send, recv, slot):
+        remote = pltpu.make_async_remote_copy(
+            source, landing, send, recv, device_id={"rows": base + slot}
+        )
+        return remote, pltpu.make_async_copy(source, landing, recv)
+
+    def send_row(source, landing, send, recv, slot):
+        remote, local = row_copy(source, landing, send, recv, slot)
+
+        @pl.when(slot != me)
+        def _():
+            remote.start()
+
+        @pl.when(slot == me)
+        def _():
+            local.start()
+
+    hop = pltpu.make_async_remote_copy(
+        xbuf.at[group],
+        xbuf.at[0],
+        hop_send,
+        hop_recv,
+        device_id={"rows": after * group + me},
+    )
+
+    ahead = jnp.where(has_before, group, 1)
+    lax.fori_loop(0, ahead, prepare, 0)
+
+    @pl.when(has_before)
+    def _():
+        pltpu.make_async_copy(xbuf.at[0], xbuf.at[0], hop_recv).wait()
+
+    @pl.when(jnp.logical_not(has_before) & (way == 0))
+    def _():
+        xbuf[0] = top_ref[column]
+
+    @pl.when(jnp.logical_not(has_before) & (way == 1))
+    def _():
+        xbuf[0] = bottom_ref[column]
+
+    for u, block in enumerate(unpack_lanes(load_tiles(xbuf, 0, width), chi)):
+        x32[u * chi : (u + 1) * chi] = block
+
+    def absorb(step, unused):
+        slot = step + way * (group - 1 - 2 * step)
+
+        @pl.when(step >= ahead)
+        def _():
+            prepare(step, 0)
+
+        send_row(
+            xbuf.at[step], env_ref.at[way, column], env_send.at[step], env_recv.at[way, column], slot
+        )
+        x_high, x_low = halves(x32[...])
+        q_high = qhi[step]
+        jbuf[...] = dot32(x_high, q_high) + (dot32(x_high, qlo[step]) + dot32(x_low, q_high))
+        chunk = 16
+
+        def through(at, unused):
+            start = pl.multiple_of(at * chunk, chunk)
+            for l in range(D2):
+                for d in range(D2):
+                    total = None
+                    for u in range(D2):
+                        for w in range(D2):
+                            ket_at = (u // D) * 8 + (l // D) * 4 + (d // D) * 2 + w // D
+                            bra_at = (u % D) * 8 + (l % D) * 4 + (d % D) * 2 + w % D
+                            spot = ket_at * 16 + bra_at
+                            term = (
+                                ebuf[step, spot : spot + 1, :]
+                                * jbuf[
+                                    pl.ds(u * chi + start, chunk), w * LANES : (w + 1) * LANES
+                                ]
+                            )
+                            total = term if total is None else total + term
+                    high, low = halves(total)
+                    rows = pl.ds(l * LANES + start, chunk)
+                    thi[rows, d * LANES : (d + 1) * LANES] = high
+                    tlo[rows, d * LANES : (d + 1) * LANES] = low
+            return unused
+
+        lax.fori_loop(0, chi // chunk, through, 0)
+        t_high = thi[...]
+        p_high = phi[step]
+        renewed = dot32(p_high, t_high) + (dot32(p_high, tlo[...]) + dot32(plo[step], t_high))
+        square = jnp.sum(jnp.sum(renewed * renewed, axis=1, keepdims=True), axis=0, keepdims=True)
+        renewed = renewed * (1.0 / jnp.sqrt(square / (chi * width) + EPSILON))
+        blocks = [renewed[:, d * LANES : (d + 1) * LANES] for d in range(D2)]
+        for d, block in enumerate(blocks):
+            x32[d * chi : (d + 1) * chi] = block
+        for t, tile in enumerate(pack_lanes(blocks, chi)):
+            xbuf[step + 1, :, t * LANES : (t + 1) * LANES] = tile
+
+        @pl.when((step == group - 1) & has_after)
+        def _():
+            hop.start()
+
+        send_row(
+            xbuf.at[step + 1],
+            out_ref.at[way, column],
+            out_send.at[step],
+            out_recv.at[way, column],
+            slot,
+        )
+        return unused
+
+    lax.fori_loop(0, group, absorb, 0)
+
+    for step in range(group):
+        slot = step + way * (group - 1 - 2 * step)
+
+        @pl.when(slot != me)
+        def _():
+            row_copy(
+                xbuf.at[step],
+                env_ref.at[way, column],
+                env_send.at[step],
+                env_recv.at[way, column],
+                slot,
+            )[0].wait_send()
+            row_copy(
+                xbuf.at[step + 1],
+                out_ref.at[way, column],
+                out_send.at[step],
+                out_recv.at[way, column],
+                slot,
+            )[0].wait_send()
+
+    for target in range(group):
+
+        @pl.when(target != me)
+        def _():
+            for copy in map_copies(target % 2, target // 2, target, False):
+                copy.wait_send()
+
+    @pl.when(has_after)
+    def _():
+        hop.wait_send()
+
+    for a in range(2):
+        for b in range(local_cols):
+            pltpu.make_async_copy(env_ref.at[a, b], env_ref.at[a, b], env_recv.at[a, b]).wait()
+            pltpu.make_async_copy(out_ref.at[a, b], out_ref.at[a, b], out_recv.at[a, b]).wait()
+
+
+def boundary_chains(row_count, kets, left_maps, right_maps, top_edge, bottom_edge):
+    local_cols = kets.shape[1]
+    chi, width = left_maps.shape[-2:]
+    group = 2 * local_cols
+    tensors = kets[0].reshape((local_cols, PHYS) + (D,) * 4)
+    both = jnp.stack([tensors, jnp.swapaxes(tensors, 2, 4)]).reshape(2, local_cols, -1)
+    spread = jnp.broadcast_to(both[..., None], both.shape + (LANES,))
+    shape = jax.ShapeDtypeStruct((2, local_cols, chi, width), jnp.float32)
+    vmem = pl.BlockSpec(memory_space=pltpu.VMEM)
+    wide = D2 * LANES
+    dma = pltpu.SemaphoreType.DMA
+    return pl.pallas_call(
+        functools.partial(chain_kernel, row_count),
+        out_shape=(shape, shape),
+        in_specs=[vmem] * 5,
+        out_specs=(vmem, vmem),
+        scratch_shapes=[
+            pltpu.VMEM((group, chi, width), jnp.float32),
+            pltpu.VMEM((group, chi, width), jnp.float32),
+            pltpu.VMEM((group,) + spread.shape[2:], jnp.float32),
+            pltpu.VMEM((group + 1, chi, width), jnp.float32),
+            pltpu.VMEM((group, D2**4, LANES), jnp.float32),
+            pltpu.VMEM((wide, width), jnp.bfloat16),
+            pltpu.VMEM((group, chi, wide), jnp.bfloat16),
+            pltpu.VMEM((group, chi, wide), jnp.bfloat16),
+            pltpu.VMEM((group, LANES, wide), jnp.bfloat16),
+            pltpu.VMEM((group, LANES, wide), jnp.bfloat16),
+            pltpu.VMEM((D2 * chi, LANES), jnp.float32),
+            pltpu.VMEM((D2 * chi, wide), jnp.float32),
+            pltpu.VMEM((wide, wide), jnp.bfloat16),
+            pltpu.VMEM((wide, wide), jnp.bfloat16),
+            dma((3, group)),
+            dma((3, group)),
+            dma((group,)),
+            dma((2, local_cols)),
+            dma((group,)),
+            dma((2, local_cols)),
+            dma,
+            dma,
+        ],
+        compiler_params=pltpu.CompilerParams(
+            collective_id=0, has_side_effects=True, vmem_limit_bytes=48 * 1024 * 1024
+        ),
+        name="chains",
+    )(spread, left_maps[:, 0], right_maps[:, 0], top_edge, bottom_edge)
 
 
 def shards(
@@ -127,89 +505,9 @@
     local_cols = kets.shape[1]
     layers = jax.vmap(jax.vmap(pair_layers))(kets)
     column_shape = (CHI, D2 * CHI)
-    blank_column = jnp.zeros(column_shape, jnp.float32)
-
-    def run_down(source, column):
-        current = source
-        current = absorb_down(
-            current,
-            select_at(layers[0], column),
-            select_at(left_maps[0, 0], column),
-            select_at(right_maps[0, 0], column),
-        )
-        columns_out = [current]
-        return jnp.stack(columns_out)
-
-    def run_up(source, column):
-        columns_out = [None] * local_rows
-        current = source
-        for local_row in reversed(range(local_rows)):
-            current = absorb_up(
-                current,
-                select_at(layers[local_row], column),
-                select_at(left_maps[1, local_row], column),
-                select_at(right_maps[1, local_row], column),
-            )
-            columns_out[local_row] = current
-        return jnp.stack(columns_out)
-
-    def pipe_step(step_number, carried):
-        from_above, from_below, enter_top, leave_top, enter_bottom, leave_bottom = carried
-        slot_top = step_number - row_place
-        column_top = jnp.clip(slot_top, 0, local_cols - 1)
-        source_top = jnp.where(row_place == 0, select_at(top_edge, column_top), from_above)
-
-        def down_live(stores):
-            renewed = run_down(source_top, column_top)
-            entered = lax.dynamic_update_index_in_dim(stores[0], source_top, column_top, 0)
-            left_now = lax.dynamic_update_index_in_dim(stores[1], renewed, column_top, 1)
-            return (entered, left_now, renewed[local_rows - 1])
-
-        def down_spare(stores):
-            return (stores[0], stores[1], blank_column)
-
-        live_top = (slot_top >= 0) & (slot_top < local_cols)
-        enter_top, leave_top, send_down = lax.cond(
-            live_top, down_live, down_spare, (enter_top, leave_top)
-        )
-        slot_bottom = step_number - (row_count - 1 - row_place)
-        column_bottom = jnp.clip(slot_bottom, 0, local_cols - 1)
-        source_bottom = jnp.where(
-            row_place == row_count - 1, select_at(bottom_edge, column_bottom), from_below
-        )
-
-        def up_live(stores):
-            renewed = run_up(source_bottom, column_bottom)
-            entered = lax.dynamic_update_index_in_dim(stores[0], source_bottom, column_bottom, 0)
-            left_now = lax.dynamic_update_index_in_dim(stores[1], renewed, column_bottom, 1)
-            return (entered, left_now, renewed[0])
-
-        def up_spare(stores):
-            return (stores[0], stores[1], blank_column)
-
-        live_bottom = (slot_bottom >= 0) & (slot_bottom < local_cols)
-        enter_bottom, leave_bottom, send_up = lax.cond(
-            live_bottom, up_live, up_spare, (enter_bottom, leave_bottom)
-        )
-        from_above = shifted(send_down, "rows", 1)
-        from_below = shifted(send_up, "rows", -1)
-        return (from_above, from_below, enter_top, leave_top, enter_bottom, leave_bottom)
-
-    entry_shape = (local_cols,) + column_shape
-    store_shape = (local_rows, local_cols) + column_shape
-    initial = (
-        blank_column,
-        blank_column,
-        jnp.zeros(entry_shape, jnp.float32),
-        jnp.zeros(store_shape, jnp.float32),
-        jnp.zeros(entry_shape, jnp.float32),
-        jnp.zeros(store_shape, jnp.float32),
-    )
-    unused_above, unused_below, enter_top, leave_top, enter_bottom, leave_bottom = lax.fori_loop(
-        0, row_count + local_cols - 1, pipe_step, initial
-    )
-    above = jnp.concatenate([enter_top[None], leave_top[:-1]], axis=0)
-    below = jnp.concatenate([leave_bottom[1:], enter_bottom[None]], axis=0)
+    outs, envs = boundary_chains(row_count, kets, left_maps, right_maps, top_edge, bottom_edge)
+    leave_top, leave_bottom = outs[0][None], outs[1][None]
+    above, below = envs[0][None], envs[1][None]
     global_rows = row_place * local_rows + jnp.arange(local_rows, dtype=jnp.int32)
     global_cols = col_place * local_cols + jnp.arange(local_cols, dtype=jnp.int32)
     row_match = term_rows[:, None] == global_rows[None, :]

time: 565 us -> 258 us (0.46)
  starting transfers between devices: 256 us -> 41.6 us
  Pallas kernels: 0 us -> 61.2 us
  matrix products: 74.9 us -> 25.7 us
  blocking collectives: 89.8 us -> 41.4 us
  loops' own time: 36.3 us -> 5.64 us
  local copies, waits for them, and re-layouts: 55.9 us -> 33.8 us
    ppermute x39 -> x5, starting transfers between devices: 256 us -> 41.6 us  [shifted(): lax.ppermute(value, axis, [(source, source + steps) for source in range(i...]
    pallas_call x0 -> x1, Pallas kernels: none -> 61.2 us  [boundary_chains(): pl.pallas_call(functools.partial(chain_kernel, row_count), out_shape=(sha...]
    dot_general x44 -> x23, matrix products: 74.5 us -> 25.3 us  [product(): jnp.einsum(pattern, former, latter, precision=PRECISION_HIGH, preferred_e...]
    psum x1, blocking collectives: 89.8 us -> 41.4 us  [shards(): energies = lax.psum(term_share, ('rows', 'cols'))]
    another operation x2, loops' own time: 15.3 us -> 1.31 us  [chain_step(): lax.cond(section_number == col_place, left_live, left_spare, left_opens)]
    broadcast_in_dim x32 -> x1, local copies, waits for them, and re-layouts: 10.9 us -> 0.08 us  [boundary_chains(): spread = jnp.broadcast_to(both[..., None], both.shape + (LANES,))]
    another operation x2, loops' own time: 7.67 us -> 1.18 us  [chain_step(): lax.cond(section_number == col_count - 1 - col_place, right_live, right_s...]
    ppermute x39 -> x5, waiting for transfers between devices: 36.8 us -> 35.2 us  [shifted(): lax.ppermute(value, axis, [(source, source + steps) for source in range(i...]
  transfers between devices with their start and end apart: 39 -> 5, of which waited for: 20 -> 4; matrix products, arithmetic and copies ran while one was open for 10% -> 7% of each run, Pallas kernels for 0% -> 0%
where the time goes in v1:
time: 258 us; the launch traced here: 254 us
  Pallas kernels  61.2 us (24%)
  starting transfers between devices  41.6 us (16%)
  blocking collectives  41.4 us (16%)
  waiting for transfers between devices  35.2 us (14%)
  local copies, waits for them, and re-layouts  33.8 us (13%)
  matrix products  25.7 us (10%)
  other arithmetic  8.56 us (3%)
  loops' own time  5.64 us (2%)
    pallas_call x1, Pallas kernels, boundary_chains(): pl.pallas_call(functools.partial(chain_kernel, row_count), out_shape=(sha...  61.2 us
    ppermute x5, starting transfers between devices, shifted(): lax.ppermute(value, axis, [(source, source + steps) for source in range(i...  41.6 us
    psum x1, blocking collectives, shards(): energies = lax.psum(term_share, ('rows', 'cols'))  41.4 us
    ppermute x5, waiting for transfers between devices, shifted(): lax.ppermute(value, axis, [(source, source + steps) for source in range(i...  35.2 us
    dot_general x23, matrix products, product(): jnp.einsum(pattern, former, latter, precision=PRECISION_HIGH, preferred_e...  25.3 us
    another operation x11, local copies, waits for them, and re-layouts  6.22 us
  transfers between devices with their start and end apart: 5, of which 4 were waited for; matrix products, arithmetic and copies ran while one was open for 7% of the time, Pallas kernels for 0%

profile of v1, /device:TPU:0, one launch (start us, length us, event | category | flops | bytes accessed | tf_op | source)
XLA Modules:
  0.0 254.2 jit_solution(15025622838977306040)
XLA Ops:
  6.4 61.2 %chains.1 = (f32[2,2,96,384]{3,2,1,0:T(8,128)S(1)}, f32[2,2,96,384]{3,2,1,0:T(8,128)S(1)}) custom-call(f32[2,2,32,128]{3,2,1,0:T(8,128)S(1)} %broadcast_in_dim.94.kets_ref, f32[2,2,96,384]{3,2,1,0:T(8,128)S(1)} %bitcast.365, f32[2,2,96,384]{3,2,1,0:T(8,128)S(1)} %bitcast.366, f32[2,96,384]{2,1,0:T(8,128)S(1)} %copy-done.3, f32[2,96,384]{2,1,0:T(8,128)S(1)} %copy-done.4), custom_call_target="tpu_custom_call" | custom-call | tf_op jit(solution)/shard_map/chains/pallas_call | solution.py:451
  73.3 119.9 %while.66 = (s32[]{:T(128)}, f32[1,96,384]{2,1,0:T(8,128)S(1)}, f32[1,96,384]{2,1,0:T(8,128)}, f32[1,2,4,96,384]{4,3,2,1,0:T(8,128)}, f32[1,2,4,96,384]{4,3,2,1,...) while((s32[]{:T(128)}, f32[1,96,384]{2,1,0:T(8,128)S(1)}, ...), condition=%wide.region_35.36_spmd, body=%wide.region_2.35_spmd.sunk | while | flops 738242560 | bytes 34500900 | solution.py:594
  73.3 32.0 %conditional.8 = (f32[1,2,4,96,384]{4,3,2,1,0:T(8,128)}, f32[1,96,384]{2,1,0:T(8,128)}) conditional(s32[]{:T(128)} %convert_element_type.46, f32[1,2,4,96,384]{4,3,2,1,0:T(8,128)} %get-tuple-element.1193, (pred[1,2]{1,0:T(4,128)(4,1)S(1)}, s32[]{:T(128)}, f32[1,96,384]{1,2,0:T(8,128)S(1)}, f32[1,96,384]{2,1,0:T(8,128)S(1)}, ...), branch_computations={%region_3.0_spmd, %region_4.18_spmd} | conditional | flops 369121280 | bytes 16072630 | solution.py:549
  76.3 6.2 %conditional = (f32[96,384]{1,0:T(8,128)S(1)}, f32[1,4,96,384]{3,2,1,0:T(8,128)}) conditional(s32[]{:T(128)} %bitcast.53, (f32[1,96,384]{1,2,0:T(8,128)S(1)}, f32[1,1,96,384]{3,2,1,0:T(8,128)S(1)}, f32[1,2,4,4,4,4]{2,5,3,4,1,0:T(4,128)}, f32[1,1,96,384]{3,2,1,0:T(8,128)S(1)}) %tuple.87, (f32[1,2,32]{2,1,0:T(2,128)S(1)}, f32[1,96,384]{1,2,0:T(8,128)S(1)}, ...), branch_computations={%region_5.5_spmd, %region_7.10_spmd} | conditional | flops 184394752 | bytes 5650565 | solution.py:90
  76.9 2.0 convolution_bitcast_fusion
  83.1 19.8 %conditional.1 = (f32[1,4,96,384]{3,2,1,0:T(8,128)}, f32[1,96,384]{2,1,0:T(8,128)}) conditional(s32[]{:T(128)} %bitcast.54, (f32[96,384]{1,0:T(8,128)S(1)}, f32[1,1,96,384]{3,2,1,0:T(8,128)S(1)}, f32[1,2,4,4,4,4]{2,5,3,4,1,0:T(4,128)}, f32[1,1,96,384]{3,2,1,0:T(8,128)S(1)}) %tuple.89, (f32[1,2,32]{2,1,0:T(2,128)S(1)}, f32[96,384]{1,0:T(8,128)S(1)}, ...), branch_computations={%region_12.12_spmd, %region_14.17_spmd} | conditional | flops 184394752 | bytes 6141577 | solution.py:90
  83.9 15.7 %while.63 = (s32[]{:T(128)}, f32[4,96,384]{2,1,0:T(8,128)}, f32[96,384]{0,1:T(8,128)S(1)}, f32[1,1,96,384]{3,2,1,0:T(8,128)S(1)}, f32[4,4,4,4,4]{1,4,2,3,0:T(4,1...) while((s32[]{:T(128)}, f32[4,96,384]{2,1,0:T(8,128)}, f32[96,384]{0,1:T(8,128)S(1)}, ...), condition=%wide.region_16.14_spmd, body=%wide.region_15.13_spmd.sunk | while | flops 184025088 | bytes 4653649 | solution.py:80
  102.9 2.3 maximum_bitcast_fusion
  108.5 2.0 collective-permute-done
  110.6 18.6 %collective-permute-done.1 = f32[1,96,384]{2,1,0:T(8,128)S(1)} collective-permute-done((f32[1,96,384]{2,1,0:T(8,128)}, f32[1,96,384]{2,1,0:T(8,128)S(1)}, u32[]{:S(2)}, u32[]{:S(2)}) %collective-permute-start.1) | collective-permute-done | bytes 147488 | tf_op jit(solution)/shard_map/while/body/eval_jaxpr/ppermute | solution.py:25
  130.5 36.5 %collective-permute-start = (f32[1,96,384]{2,1,0:T(8,128)}, f32[1,96,384]{2,1,0:T(8,128)S(1)}, u32[]{:S(2)}, u32[]{:S(2)}) collective-permute-start(f32[1,96,384]{2,1,0:T(8,128)} %get-tuple-element.1038), channel_id=1, source_target_pairs={{0,1},{2,3},{4,5},{6,7},{8,9},{10,11},{12,13},{14,15},{16,17},{18,... | collective-permute-start | bytes 442376 | tf_op jit(solution)/shard_map/while/body/eval_jaxpr/ppermute | solution.py:25
  167.0 18.2 %conditional.9 = (f32[1,2,4,96,384]{4,3,2,1,0:T(8,128)}, f32[1,96,384]{2,1,0:T(8,128)}) conditional(s32[]{:T(128)} %convert_element_type.47, f32[1,2,4,96,384]{4,3,2,1,0:T(8,128)} %get-tuple-element.1194, (pred[1,2]{1,0:T(4,128)(4,1)S(1)}, s32[]{:T(128)}, f32[1,96,384]{1,2,0:T(8,128)S(1)}, f32[1,96,384]{2,1,0:T(8,128)}, ...), branch_computations={%region_19.19_spmd, %region_20.34_spmd} | conditional | flops 369121280 | bytes 16658386 | solution.py:576
  169.2 6.1 %conditional.2 = (f32[96,384]{1,0:T(8,128)S(1)}, f32[1,4,96,384]{3,2,1,0:T(8,128)}) conditional(s32[]{:T(128)} %bitcast.110, (f32[1,96,384]{1,2,0:T(8,128)S(1)}, f32[1,1,96,384]{3,2,1,0:T(8,128)S(1)}, f32[1,2,4,4,4,4]{2,4,5,3,1,0:T(4,128)}, f32[1,1,96,384]{3,2,1,0:T(8,128)S(1)}) %tuple.101, (f32[1,2,32]{2,1,0:T(2,128)S(1)}, ...), branch_computations={%region_21.21_spmd, %region_23.26_spmd} | conditional | flops 184394752 | bytes 5650565 | solution.py:90
  169.9 2.0 convolution_bitcast_fusion.12
  175.9 7.0 %conditional.3 = (f32[1,4,96,384]{3,2,1,0:T(8,128)}, f32[1,96,384]{2,1,0:T(8,128)}) conditional(s32[]{:T(128)} %bitcast.109, (f32[96,384]{1,0:T(8,128)S(1)}, f32[1,1,96,384]{3,2,1,0:T(8,128)S(1)}, f32[1,2,4,4,4,4]{2,4,5,3,1,0:T(4,128)}, f32[1,1,96,384]{3,2,1,0:T(8,128)S(1)}) %tuple.103, (f32[1,2,32]{2,1,0:T(2,128)S(1)}, f32[96,384]{1,0:T(8,128)S(1)}, ...), branch_computations={%region_28.28_spmd, %region_30.33_spmd} | conditional | flops 184394752 | bytes 6141577 | solution.py:90
  176.8 2.0 convolution_bitcast_fusion.18
  179.0 1.5 multiply_reduce_fusion.3
  182.9 2.4 maximum_bitcast_fusion.1
  186.6 5.9 %collective-permute-done.1 = f32[1,96,384]{2,1,0:T(8,128)S(1)} collective-permute-done((f32[1,96,384]{2,1,0:T(8,128)}, f32[1,96,384]{2,1,0:T(8,128)S(1)}, u32[]{:S(2)}, u32[]{:S(2)}) %collective-permute-start.1) | collective-permute-done | bytes 147488 | tf_op jit(solution)/shard_map/while/body/eval_jaxpr/ppermute | solution.py:25
  193.2 2.2 fusion.98
  196.9 1.8 reshape.453
  198.8 8.6 %collective-permute-done.2 = f32[1,4,96,384]{3,2,1,0:T(8,128)} collective-permute-done((f32[1,4,96,384]{3,2,1,0:T(8,128)}, f32[1,4,96,384]{3,2,1,0:T(8,128)}, u32[]{:S(2)}, u32[]{:S(2)}) %collective-permute-start.2) | collective-permute-done | bytes 589856 | tf_op jit(solution)/shard_map/ppermute | solution.py:25
  208.8 2.4 multiply_reduce_fusion.13
  212.7 41.4 %psum.7 = f32[16]{0:T(128)} all-reduce(f32[16]{0:T(128)S(1)} %fusion.72), channel_id=1, replica_groups=mesh['rows'=16,'cols'=2] {'rows','cols'}, use_global_device_ids=true, to_apply=%region_39.40 | all-reduce | flops 16 | bytes 128 | tf_op jit(solution)/shard_map/psum | solution.py:618
  (153 shorter events, 55.9 us)
Async XLA Ops:
  0.6 210.9 %copy-start = (f32[4,16]{1,0:T(4,128)S(1)}, f32[4,16]{1,0:T(4,128)}, u32[]{:S(2)}) copy-start(f32[4,16]{1,0:T(4,128)} %param.43) | copy-start | bytes 772
  0.7 69.5 %copy-start.12 = (s32[2]{0:T(128)}, s32[2]{0:T(128)S(1)}, u32[]{:S(2)}) copy-start(s32[2]{0:T(128)S(1)} %get-tuple-element.817) | copy-start | bytes 28
  2.3 1.1 copy-start.1
  3.4 1.1 copy-start.2
  4.5 1.0 copy-start.3
  5.4 1.0 copy-start.4
  67.6 2.2 copy-start.7
  67.6 2.3 copy-start.8
  67.6 2.4 copy-start.16
  67.6 2.5 copy-start.10
  70.1 1.4 copy-start.14
  70.4 3.0 %copy-start.9 = (f32[1,2,32]{2,1,0:T(2,128)S(1)}, f32[1,2,32]{2,1,0:T(2,128)}, u32[]{:S(2)}) copy-start(f32[1,2,32]{2,1,0:T(2,128)} %param.33) | copy-start | bytes 772
  105.3 5.3 %collective-permute-start = (f32[1,96,384]{2,1,0:T(8,128)}, f32[1,96,384]{2,1,0:T(8,128)S(1)}, u32[]{:S(2)}, u32[]{:S(2)}) collective-permute-start(f32[1,96,384]{2,1,0:T(8,128)} %get-tuple-element.1038), channel_id=1, source_target_pairs={{0,1},{2,3},{4,5},{6,7},{8,9},{10,11},{12,13},{14,15},{16,17},{18,... | collective-permute-start | bytes 442376 | tf_op jit(solution)/shard_map/while/body/eval_jaxpr/ppermute | solution.py:25
  107.2 22.0 %collective-permute-start.1 = (f32[1,96,384]{2,1,0:T(8,128)}, f32[1,96,384]{2,1,0:T(8,128)S(1)}, u32[]{:S(2)}, u32[]{:S(2)}) collective-permute-start(f32[1,96,384]{2,1,0:T(8,128)} %get-tuple-element.1039), channel_id=1, source_target_pairs={{1,0},{3,2},{5,4},{7,6},{9,8},{11,10},{13,12},{15,14},{17,16},{19,... | collective-permute-start | bytes 442376 | tf_op jit(solution)/shard_map/while/body/eval_jaxpr/ppermute | solution.py:25
  129.2 0.7 copy-start.6
  130.5 56.0 %collective-permute-start = (f32[1,96,384]{2,1,0:T(8,128)}, f32[1,96,384]{2,1,0:T(8,128)S(1)}, u32[]{:S(2)}, u32[]{:S(2)}) collective-permute-start(f32[1,96,384]{2,1,0:T(8,128)} %get-tuple-element.1038), channel_id=1, source_target_pairs={{0,1},{2,3},{4,5},{6,7},{8,9},{10,11},{12,13},{14,15},{16,17},{18,... | collective-permute-start | bytes 442376 | tf_op jit(solution)/shard_map/while/body/eval_jaxpr/ppermute | solution.py:25
  167.1 0.9 copy-start.5
  185.3 7.2 %collective-permute-start.1 = (f32[1,96,384]{2,1,0:T(8,128)}, f32[1,96,384]{2,1,0:T(8,128)S(1)}, u32[]{:S(2)}, u32[]{:S(2)}) collective-permute-start(f32[1,96,384]{2,1,0:T(8,128)} %get-tuple-element.1039), channel_id=1, source_target_pairs={{1,0},{3,2},{5,4},{7,6},{9,8},{11,10},{13,12},{15,14},{17,16},{19,... | collective-permute-start | bytes 442376 | tf_op jit(solution)/shard_map/while/body/eval_jaxpr/ppermute | solution.py:25
  192.5 0.7 copy-start.6
  195.3 12.1 %collective-permute-start.2 = (f32[1,4,96,384]{3,2,1,0:T(8,128)}, f32[1,4,96,384]{3,2,1,0:T(8,128)}, u32[]{:S(2)}, u32[]{:S(2)}) collective-permute-start(f32[1,4,96,384]{3,2,1,0:T(8,128)} %get-tuple-element.811), channel_id=1, source_target_pairs={{1,0},{3,2},{5,4},{7,6},{9,8},{11,10},{13,12},{15,14},{17,16},{19,... | collective-permute-start | bytes 1769480 | tf_op jit(solution)/shard_map/ppermute | solution.py:25
  208.7 2.6 %copy-start.11 = (s32[16]{0:T(128)S(1)}, s32[16]{0:T(128)}, u32[]{:S(2)}) copy-start(s32[16]{0:T(128)} %param.41) | copy-start | bytes 196
  208.7 2.6 %copy-start.13 = (s32[2]{0:T(128)S(1)}, s32[2]{0:T(128)}, u32[]{:S(2)}) copy-start(s32[2]{0:T(128)} %copy-done.12) | copy-start | bytes 28
  208.8 2.6 %copy-start.15 = (pred[16]{0:T(512)(128)(4,1)S(1)}, pred[16]{0:T(512)(128)(4,1)}, u32[]{:S(2)}) copy-start(pred[16]{0:T(512)(128)(4,1)} %copy-done.14) | copy-start | bytes 52
  208.8 2.8 %copy-start.17 = (s32[16]{0:T(128)S(1)}, s32[16]{0:T(128)}, u32[]{:S(2)}) copy-start(s32[16]{0:T(128)} %param.42) | copy-start | bytes 196

commit v2 on v1

--- a/solution.py
+++ b/solution.py
@@ -16,78 +16,6 @@
 
 
 EPSILON = 1e-06
-PRECISION_HIGH = lax.Precision.HIGH
-
-
-def shifted(value, axis, steps):
-    count = lax.axis_size(axis)
-    initial, last = (max(0, -steps), min(count, count - steps))
-    return lax.ppermute(value, axis, [(source, source + steps) for source in range(initial, last)])
-
-
-def product(pattern, former, latter):
-    return jnp.einsum(
-        pattern, former, latter, precision=PRECISION_HIGH, preferred_element_type=jnp.float32
-    )
-
-
-def normalize(values):
-    return values / jnp.sqrt(jnp.mean(values * values) + EPSILON)
-
-
-def select_at(values, position):
-    return lax.dynamic_index_in_dim(values, position, 0, keepdims=False)
-
-
-def pair_layers(ket_flat):
-    tensor = ket_flat.reshape(PHYS, D, D, D, D)
-    doubled = product("pabcd,pefgh->aebfcgdh", tensor, tensor)
-    return doubled.reshape(D2, D2, D2, D2)
-
-
-def open_layers(ket_flat):
-    tensor = ket_flat.reshape(PHYS, D, D, D, D)
-    doubled = product("pabcd,qefgh->pqaebfcgdh", tensor, tensor)
-    return doubled.reshape(PHYS * PHYS, D2, D2, D2, D2)
-
-
-def pair_diagonal():
-    matched = jnp.arange(PHYS)[:, None] == jnp.arange(PHYS)[None, :]
-    return jnp.where(matched, 1.0, 0.0).astype(jnp.float32).reshape(PHYS * PHYS)
-
-
-def left_core(environ, layers, above_col, below_col):
-    env_three = environ.reshape(CHI, D2, CHI)
-    upper_three = above_col.reshape(CHI, D2, CHI)
-    lower_three = below_col.reshape(CHI, D2, CHI)
-    step_one = product("alb,aux->lbux", env_three, upper_three)
-    step_two = product("lbux,uldr->bxdr", step_one, layers)
-    return product("bxdr,bdy->xry", step_two, lower_three).reshape(CHI, D2 * CHI)
-
-
-def right_core(environ, layers, above_col, below_col):
-    env_three = environ.reshape(CHI, D2, CHI)
-    upper_three = above_col.reshape(CHI, D2, CHI)
-    lower_three = below_col.reshape(CHI, D2, CHI)
-    step_one = product("xry,aux->ryau", env_three, upper_three)
-    step_two = product("ryau,uldr->yald", step_one, layers)
-    return product("yald,bdy->alb", step_two, lower_three).reshape(CHI, D2 * CHI)
-
-
-def side_step(core_map, environ, ket_flat, layers, above_col, below_col, wanted):
-
-    def with_open(unused):
-        opened = lax.map(
-            lambda single: core_map(environ, single, above_col, below_col), open_layers(ket_flat)
-        )
-        closed = jnp.sum(pair_diagonal()[:, None, None] * opened, axis=0)
-        return (opened, normalize(closed))
-
-    def without_open(unused):
-        empty_open = jnp.zeros((PHYS * PHYS, CHI, D2 * CHI), jnp.float32)
-        return (empty_open, normalize(core_map(environ, layers, above_col, below_col)))
-
-    return lax.cond(wanted, with_open, without_open, 0)
 
 
 LANES = 128
@@ -484,6 +412,380 @@
     )(spread, left_maps[:, 0], right_maps[:, 0], top_edge, bottom_edge)
 
 
+def environment_kernel(
+    row_count,
+    col_count,
+    kets_ref,
+    above_ref,
+    below_ref,
+    left_ref,
+    right_ref,
+    rows_ref,
+    bonds_ref,
+    ops_ref,
+    energy_ref,
+    near,
+    far,
+    vbuf,
+    jbuf,
+    thi,
+    tlo,
+    opens,
+    hop_out,
+    hop_in,
+    half_in,
+    shares,
+    row_share,
+    hop_send,
+    hop_recv,
+    half_send,
+    half_recv,
+    share_send,
+    share_recv,
+):
+    local_cols = above_ref.shape[0]
+    chi, width = above_ref.shape[1:]
+    half = chi // 2
+    rows_at = lax.axis_index("rows")
+    cols_at = lax.axis_index("cols")
+    has_left = cols_at > 0
+    has_right = cols_at < col_count - 1
+    pairs = PHYS * PHYS
+
+    barrier = pltpu.get_barrier_semaphore()
+    for other in range(row_count):
+
+        @pl.when(rows_at != other)
+        def _():
+            pl.semaphore_signal(barrier, inc=1, device_id={"rows": other})
+
+    for other in range(col_count):
+
+        @pl.when(cols_at != other)
+        def _():
+            pl.semaphore_signal(barrier, inc=1, device_id={"cols": other})
+
+    thi[...] = jnp.zeros_like(thi)
+    tlo[...] = jnp.zeros_like(tlo)
+    vbuf[...] = jnp.zeros_like(vbuf)
+    unit = jnp.where(
+        lax.broadcasted_iota(jnp.int32, (LANES, LANES), 0)
+        == lax.broadcasted_iota(jnp.int32, (LANES, LANES), 1),
+        1.0,
+        0.0,
+    ).astype(jnp.bfloat16)
+    fill = jnp.zeros((LANES - chi, LANES), jnp.bfloat16)
+    for column in range(local_cols):
+        for source, flipped_side, is_near in ((above_ref, 0, True), (below_ref, 1, False)):
+            blocks = unpack_lanes(load_tiles(source, column, width), chi)
+            for at, block in enumerate(blocks):
+                lanes = slice(at * LANES, (at + 1) * LANES)
+                for part, values in enumerate(halves(block)):
+                    tall = jnp.concatenate([values, fill], axis=0)
+                    turned = dot_last(unit, tall).astype(jnp.bfloat16)
+                    if is_near:
+                        rows = slice(part * chi, (part + 1) * chi)
+                        near[flipped_side, column, rows, lanes] = turned[:chi]
+                        near[1 - flipped_side, column, rows, lanes] = values
+                    else:
+                        far[flipped_side, column, part, :, lanes] = turned
+                        far[1 - flipped_side, column, part, :, lanes] = tall
+
+    pl.semaphore_wait(barrier, row_count - 1 + col_count - 1)
+
+    late = jnp.where(cols_at >= col_count // 2, 1, 0)
+
+    def hop(side, step):
+        return pltpu.make_async_remote_copy(
+            hop_out.at[side],
+            hop_in.at[side],
+            hop_send.at[side],
+            hop_recv.at[side],
+            device_id={"cols": cols_at + step},
+        )
+
+    def half_copy(side):
+        start, column, step = ((half, local_cols - 1, 1), (0, 0, -1))[side]
+        return pltpu.make_async_remote_copy(
+            opens.at[side, column, :, pl.ds(start, half)],
+            half_in.at[side],
+            half_send.at[side],
+            half_recv.at[side],
+            device_id={"cols": cols_at + step},
+        )
+
+    def put_environ(blocks):
+        for at, block in enumerate(blocks):
+            vbuf[at * chi : (at + 1) * chi] = block
+
+    def walk(turn, unused):
+        side = (turn // local_cols + late) % 2
+        order = turn % local_cols
+        column = order + side * (local_cols - 1 - 2 * order)
+        first = ((side == 0) & (cols_at == 0)) | ((side == 1) & (cols_at == col_count - 1))
+        final = ((side == 1) & (cols_at == 0)) | ((side == 0) & (cols_at == col_count - 1))
+        ending = order == local_cols - 1
+
+        @pl.when((order == 0) & jnp.logical_not(first))
+        def _():
+            pltpu.make_async_copy(hop_in.at[side], hop_in.at[side], hop_recv.at[side]).wait()
+            put_environ(unpack_lanes(load_tiles(hop_in, side, width), chi))
+
+        for at, edge in enumerate((left_ref, right_ref)):
+
+            @pl.when((order == 0) & first & (side == at))
+            def _():
+                put_environ(unpack_lanes(load_tiles(edge, 0, width), chi))
+
+        @pl.when(jnp.logical_not(ending & final))
+        def _():
+            v_high, v_low = halves(vbuf[...])
+            f_high = far[side, column, 0]
+            jbuf[...] = dot32(v_high, f_high) + (
+                dot32(v_high, far[side, column, 1]) + dot32(v_low, f_high)
+            )
+            chunk = 16
+
+            def ket(p, u, i, d, o):
+                at = p * 16 + u * 8 + i * 4 + d * 2 + o
+                return kets_ref[side, column, at : at + 1, :]
+
+            def through(at, unused):
+                start = pl.multiple_of(at * chunk, chunk)
+
+                def joined(i, d):
+                    return jbuf[pl.ds(i * chi + start, chunk), d * LANES : (d + 1) * LANES]
+
+                for p in range(PHYS):
+                    for u in range(D):
+                        for o in range(D):
+                            part = {}
+                            for i2 in range(D):
+                                for d2 in range(D):
+                                    total = None
+                                    for i in range(D):
+                                        for d in range(D):
+                                            term = ket(p, u, i, d, o) * joined(
+                                                i * D + i2, d * D + d2
+                                            )
+                                            total = term if total is None else total + term
+                                    part[i2, d2] = total
+                            for q in range(PHYS):
+                                for u2 in range(D):
+                                    for o2 in range(D):
+                                        total = None
+                                        for i2 in range(D):
+                                            for d2 in range(D):
+                                                term = ket(q, u2, i2, d2, o2) * part[i2, d2]
+                                                total = term if total is None else total + term
+                                        high, low = halves(total)
+                                        rows = pl.ds((u * D + u2) * LANES + start, chunk)
+                                        spot = (p * PHYS + q) * D2 + o * D + o2
+                                        lanes = slice(spot * LANES, (spot + 1) * LANES)
+                                        thi[rows, lanes] = high
+                                        tlo[rows, lanes] = low
+                return unused
+
+            lax.fori_loop(0, chi // chunk, through, 0)
+            both = near[side, column]
+            wide = D2 * LANES
+            closed = None
+            for pair in range(pairs):
+                lanes = slice(pair * wide, (pair + 1) * wide)
+                large = dot32(both, thi[:, lanes])
+                value = large[:chi] + (large[chi:] + dot32(both[:chi], tlo[:, lanes]))
+                opens[side, column, pair] = value
+                if pair // PHYS == pair % PHYS:
+                    closed = value if closed is None else closed + value
+            square = jnp.sum(
+                jnp.sum(closed * closed, axis=1, keepdims=True), axis=0, keepdims=True
+            )
+            closed = closed * (1.0 / jnp.sqrt(square / (chi * width) + EPSILON))
+            blocks = [closed[:, d * LANES : (d + 1) * LANES] for d in range(D2)]
+            put_environ(blocks)
+
+            @pl.when(ending)
+            def _():
+                for t, tile in enumerate(pack_lanes(blocks, chi)):
+                    hop_out[side, :, t * LANES : (t + 1) * LANES] = tile
+
+            for at, step in enumerate((1, -1)):
+
+                @pl.when(ending & (side == at))
+                def _():
+                    hop(at, step).start()
+                    half_copy(at).start()
+
+        return unused
+
+    lax.fori_loop(0, 2 * local_cols, walk, 0)
+
+    lane = lax.broadcasted_iota(jnp.int32, rows_ref.shape, 1)
+
+    def density(former, latter):
+        total = jnp.zeros(rows_ref.shape, jnp.float32)
+        for p in range(pairs):
+            mine = former(p)
+            for q in range(pairs):
+                value = jnp.sum(
+                    jnp.sum(mine * latter(q), axis=0, keepdims=True), axis=1, keepdims=True
+                )
+                total = jnp.where(lane == p * pairs + q, value, total)
+        return total
+
+    def share(bond, values):
+        hit = (rows_ref[...] == rows_at) & (bonds_ref[...] == bond)
+        return jnp.where(hit, values, 0.0)
+
+    mine = shares.at[cols_at]
+    mine[...] = jnp.zeros_like(rows_ref, jnp.float32)
+    for column in range(local_cols - 1):
+        mine[...] += share(
+            cols_at * local_cols + column,
+            density(lambda p: opens[0, column, p], lambda q: opens[1, column + 1, q]),
+        )
+
+    def land(side):
+        pltpu.make_async_copy(half_in.at[side], half_in.at[side], half_recv.at[side]).wait()
+
+    @pl.when(has_right)
+    def _():
+        land(1)
+        mine[...] += share(
+            cols_at * local_cols + local_cols - 1,
+            density(lambda p: opens[0, local_cols - 1, p, :half], lambda q: half_in[1, q]),
+        )
+
+    @pl.when(has_left)
+    def _():
+        land(0)
+        mine[...] += share(
+            cols_at * local_cols - 1,
+            density(lambda p: half_in[0, p], lambda q: opens[1, 0, q, half:]),
+        )
+
+    def spread(buffer, stage, axis, place, count):
+        def copies(other):
+            return pltpu.make_async_remote_copy(
+                buffer.at[place],
+                buffer.at[place],
+                share_send.at[stage, other],
+                share_recv.at[stage, place],
+                device_id={axis: other},
+            )
+
+        for other in range(count):
+
+            @pl.when(place != other)
+            def _():
+                copies(other).start()
+
+        for other in range(count):
+
+            @pl.when(place != other)
+            def _():
+                pltpu.make_async_copy(
+                    buffer.at[other], buffer.at[other], share_recv.at[stage, other]
+                ).wait()
+
+        total = buffer[0]
+        for other in range(1, count):
+            total += buffer[other]
+
+        def finish():
+            for other in range(count):
+
+                @pl.when(place != other)
+                def _():
+                    copies(other).wait_send()
+
+        return total, finish
+
+    total, finish_cols = spread(shares, 0, "cols", cols_at, col_count)
+    row_share[rows_at] = total
+    total, finish_rows = spread(row_share, 1, "rows", rows_at, row_count)
+    picked = jnp.sum(total * ops_ref[...], axis=1, keepdims=True)
+    bra, ket_at = lane % pairs, lane // pairs
+    diagonal = (bra // PHYS == bra % PHYS) & (ket_at // PHYS == ket_at % PHYS)
+    trace = jnp.sum(
+        jnp.where(diagonal & (lane < pairs * pairs), total, 0.0), axis=1, keepdims=True
+    )
+    size = jnp.sqrt(jnp.sum(total * total, axis=1, keepdims=True))
+    energy = picked / jnp.maximum(jnp.abs(trace), 0.25 * size)
+    energy_ref[...] = jnp.broadcast_to(energy, energy_ref.shape)
+    finish_cols()
+    finish_rows()
+
+    @pl.when(has_right)
+    def _():
+        hop(0, 1).wait_send()
+        half_copy(0).wait_send()
+
+    @pl.when(has_left)
+    def _():
+        hop(1, -1).wait_send()
+        half_copy(1).wait_send()
+
+
+def term_energies(
+    row_count, col_count, kets, above, below, left_edge, right_edge, rows, bonds, ops, operators
+):
+    local_cols, chi, width = above.shape
+    tensors = kets[0].reshape((local_cols, PHYS) + (D,) * 4)
+    both = jnp.stack([tensors, jnp.swapaxes(tensors, 3, 5)]).reshape(2, local_cols, -1)
+    spread = jnp.broadcast_to(both[..., None], both.shape + (LANES,))
+    terms = rows.shape[0]
+    picked = jnp.zeros((terms, LANES), jnp.float32)
+    chosen = ops[:, None, None] == jnp.arange(operators.shape[0], dtype=jnp.int32)[None, :, None]
+    chosen = jnp.sum(jnp.where(chosen, operators[None], 0.0), axis=1)
+    picked = jnp.pad(chosen, ((0, 0), (0, LANES - chosen.shape[1])))
+    tall = (terms, LANES)
+    vmem = pl.BlockSpec(memory_space=pltpu.VMEM)
+    wide = D2 * LANES
+    pairs = PHYS * PHYS
+    dma = pltpu.SemaphoreType.DMA
+    energy = pl.pallas_call(
+        functools.partial(environment_kernel, row_count, col_count),
+        out_shape=jax.ShapeDtypeStruct(tall, jnp.float32),
+        in_specs=[vmem] * 8,
+        out_specs=vmem,
+        scratch_shapes=[
+            pltpu.VMEM((2, local_cols, 2 * chi, wide), jnp.bfloat16),
+            pltpu.VMEM((2, local_cols, 2, LANES, wide), jnp.bfloat16),
+            pltpu.VMEM((D2 * chi, LANES), jnp.float32),
+            pltpu.VMEM((D2 * chi, wide), jnp.float32),
+            pltpu.VMEM((wide, pairs * wide), jnp.bfloat16),
+            pltpu.VMEM((wide, pairs * wide), jnp.bfloat16),
+            pltpu.VMEM((2, local_cols, pairs, chi, wide), jnp.float32),
+            pltpu.VMEM((2, chi, width), jnp.float32),
+            pltpu.VMEM((2, chi, width), jnp.float32),
+            pltpu.VMEM((2, pairs, chi // 2, wide), jnp.float32),
+            pltpu.VMEM((col_count,) + tall, jnp.float32),
+            pltpu.VMEM((row_count,) + tall, jnp.float32),
+            dma((2,)),
+            dma((2,)),
+            dma((2,)),
+            dma((2,)),
+            dma((2, max(row_count, col_count))),
+            dma((2, max(row_count, col_count))),
+        ],
+        compiler_params=pltpu.CompilerParams(
+            collective_id=1, has_side_effects=True, vmem_limit_bytes=48 * 1024 * 1024
+        ),
+        name="environments",
+    )(
+        spread,
+        above,
+        below,
+        left_edge,
+        right_edge,
+        jnp.broadcast_to(rows[:, None], tall),
+        jnp.broadcast_to(bonds[:, None], tall),
+        picked,
+    )
+    return energy[:, 0]
+
+
 def shards(
     kets,
     left_maps,
@@ -498,125 +800,22 @@
     operators,
 ):
     row_count = lax.axis_size("rows")
-    row_place = lax.axis_index("rows")
     col_count = lax.axis_size("cols")
-    col_place = lax.axis_index("cols")
-    local_rows = kets.shape[0]
-    local_cols = kets.shape[1]
-    layers = jax.vmap(jax.vmap(pair_layers))(kets)
-    column_shape = (CHI, D2 * CHI)
     outs, envs = boundary_chains(row_count, kets, left_maps, right_maps, top_edge, bottom_edge)
-    leave_top, leave_bottom = outs[0][None], outs[1][None]
-    above, below = envs[0][None], envs[1][None]
-    global_rows = row_place * local_rows + jnp.arange(local_rows, dtype=jnp.int32)
-    global_cols = col_place * local_cols + jnp.arange(local_cols, dtype=jnp.int32)
-    row_match = term_rows[:, None] == global_rows[None, :]
-    site_match = row_match[:, :, None] & (term_bonds[:, None, None] == global_cols[None, None, :])
-    left_need = jnp.any(site_match, axis=0)
-    right_need = jnp.any(
-        row_match[:, :, None] & (term_bonds[:, None, None] == global_cols[None, None, :] - 1),
-        axis=0,
+    energies = term_energies(
+        row_count,
+        col_count,
+        kets,
+        envs[0],
+        envs[1],
+        left_edge,
+        right_edge,
+        term_rows,
+        term_bonds,
+        term_ops,
+        operators,
     )
-    rows_shape = (local_rows,) + column_shape
-    edge_shape = (local_rows, PHYS * PHYS) + column_shape
-    open_shape = (local_rows, local_cols, PHYS * PHYS) + column_shape
-
-    def chain_step(section_number, carried):
-        from_left, from_right, edge_in, left_opens, right_opens, edge_open = carried
-
-        def left_live(stores):
-            source = jnp.where(col_place == 0, left_edge, from_left)
-            environ = source[0]
-            row_open = []
-            for column in range(local_cols):
-                opened, environ = side_step(
-                    left_core,
-                    environ,
-                    kets[0, column],
-                    layers[0, column],
-                    above[0, column],
-                    below[0, column],
-                    left_need[0, column],
-                )
-                row_open.append(opened)
-            opened_rows = [jnp.stack(row_open)]
-            sent_rows = [environ]
-            return (jnp.stack(opened_rows), jnp.stack(sent_rows))
-
-        def left_spare(stores):
-            return (stores, jnp.zeros(rows_shape, jnp.float32))
-
-        left_opens, sent_left = lax.cond(
-            section_number == col_place, left_live, left_spare, left_opens
-        )
-
-        def right_live(stores):
-            source = jnp.where(col_place == col_count - 1, right_edge, from_right)
-            environ = source[0]
-            row_open = [None] * local_cols
-            for column in reversed(range(local_cols)):
-                opened, environ = side_step(
-                    right_core,
-                    environ,
-                    kets[0, column],
-                    layers[0, column],
-                    above[0, column],
-                    below[0, column],
-                    right_need[0, column],
-                )
-                row_open[column] = opened
-            opened_rows = [jnp.stack(row_open)]
-            sent_rows = [environ]
-            kept_edge = stores[1]
-            return (jnp.stack(opened_rows), kept_edge, jnp.stack(sent_rows))
-
-        def right_spare(stores):
-            return (stores[0], stores[1], jnp.zeros(rows_shape, jnp.float32))
-
-        right_opens, edge_open, sent_right = lax.cond(
-            section_number == col_count - 1 - col_place,
-            right_live,
-            right_spare,
-            (right_opens, edge_open),
-        )
-        from_left = shifted(sent_left, "cols", 1)
-        from_right = shifted(sent_right, "cols", -1)
-        return (from_left, from_right, edge_in, left_opens, right_opens, edge_open)
-
-    chain_start = (
-        jnp.zeros(rows_shape, jnp.float32),
-        jnp.zeros(rows_shape, jnp.float32),
-        jnp.zeros(edge_shape, jnp.float32),
-        jnp.zeros(open_shape, jnp.float32),
-        jnp.zeros(open_shape, jnp.float32),
-        jnp.zeros(edge_shape, jnp.float32),
-    )
-    unused_left, unused_right, unused_edge, left_opens, right_opens, edge_open = lax.fori_loop(
-        0, col_count, chain_step, chain_start
-    )
-    edge_open = shifted(right_opens[:, 0], "cols", -1)
-    partner = jnp.concatenate([right_opens[:, 1:], edge_open[:, None]], axis=1)
-    flat_left = left_opens.reshape(local_rows * local_cols, PHYS * PHYS, -1)
-    flat_right = partner.reshape(local_rows * local_cols, PHYS * PHYS, -1)
-    density = product("kpz,kqz->kpq", flat_left, flat_right).reshape(local_rows * local_cols, -1)
-    diagonal = pair_diagonal()
-    weights = jnp.outer(diagonal, diagonal).reshape(-1)
-    trace_value = jnp.sum(density * weights[None, :], axis=1)
-    spread = jnp.sqrt(jnp.sum(density * density, axis=1))
-    valid_bond = left_need.reshape(-1)
-    denominator = jnp.where(valid_bond, jnp.maximum(jnp.abs(trace_value), 0.25 * spread), 1.0)
-    scaled = density / denominator[:, None]
-    chooser = jnp.where(site_match.reshape(TERMS, -1), 1.0, 0.0).astype(jnp.float32)
-    chosen = jnp.dot(chooser, scaled, precision=PRECISION_HIGH, preferred_element_type=jnp.float32)
-    op_match = jnp.where(
-        term_ops[:, None] == jnp.arange(OPS, dtype=jnp.int32)[None, :], 1.0, 0.0
-    ).astype(jnp.float32)
-    picked = jnp.dot(
-        op_match, operators, precision=PRECISION_HIGH, preferred_element_type=jnp.float32
-    )
-    term_share = jnp.sum(chosen * picked, axis=1)
-    energies = lax.psum(term_share, ("rows", "cols"))
-    return (leave_top, leave_bottom, energies)
+    return (outs[0][None], outs[1][None], energies)
 
 
 def solution(mesh):

time: 258 us -> 104 us (0.40); the launches traced: 254 us -> 104 us
  starting transfers between devices: 41.6 us -> 0 us
  blocking collectives: 41.4 us -> 0 us
  waiting for transfers between devices: 35.2 us -> 0 us
  Pallas kernels: 61.2 us -> 93.6 us
  matrix products: 25.7 us -> 0 us
  local copies, waits for them, and re-layouts: 33.8 us -> 9.63 us
  other arithmetic: 8.56 us -> 0.09 us
  loops' own time: 5.64 us -> 0 us
    ppermute x5 -> x0, starting transfers between devices: 41.6 us -> none  [shifted(): lax.ppermute(value, axis, [(source, source + steps) for source in range(i...]
    psum x1 -> x0, blocking collectives: 41.4 us -> none  [shards(): energies = lax.psum(term_share, ('rows', 'cols'))]
    ppermute x5 -> x0, waiting for transfers between devices: 35.2 us -> none  [shifted(): lax.ppermute(value, axis, [(source, source + steps) for source in range(i...]
    pallas_call x0 -> x1, Pallas kernels: none -> 32.8 us  [term_energies(): pl.pallas_call(functools.partial(environment_kernel, row_count, col_count...]
    dot_general x25 -> x0, matrix products: 25.7 us -> none  [the longest x23 25.3 us: product(): jnp.einsum(pattern, former, latter, precision=PRECISION_HIGH, preferred_e...]
    another operation x14 -> x1, local copies, waits for them, and re-layouts: 8.81 us -> 0.1 us  [term_energies(): jnp.stack([tensors, jnp.swapaxes(tensors, 3, 5)]).reshape(2, local_cols, -1)]
    another operation x10 -> x0, loops' own time: 5.64 us -> none  [the longest x4 2.85 us: side_step(): return lax.cond(wanted, with_open, without_open, 0)]
    another operation x3 -> x0, other arithmetic: 4.71 us -> none  [the longest x1 2.38 us: right_live(): return (jnp.stack(opened_rows), kept_edge, jnp.stack(sent_rows))]
  transfers between devices with their start and end apart: 5 -> 0, of which waited for: 4 -> 0; matrix products, arithmetic and copies ran while one was open for 7% -> 0% of each run, Pallas kernels for 0% -> 0%
where the time goes in v2:
time: 104 us
  Pallas kernels  93.6 us (90%)
  local copies, waits for them, and re-layouts  9.63 us (9%)
    pallas_call x1, Pallas kernels, boundary_chains(): pl.pallas_call(functools.partial(chain_kernel, row_count), out_shape=(sha...  60.8 us
    pallas_call x1, Pallas kernels, term_energies(): pl.pallas_call(functools.partial(environment_kernel, row_count, col_count...  32.8 us
    unnamed x22, local copies, waits for them, and re-layouts  6.64 us

profile of v2, /device:TPU:0, one launch (start us, length us, event | category | flops | bytes accessed | tf_op | source)
XLA Modules:
  0.0 104.0 jit_solution(5684325059218378830)
XLA Ops:
  0.6 0.8 reshape_squeeze.4
  1.4 0.1 stack.15
  1.5 0.2 copy.19
  1.7 0.1 stack.17
  1.8 0.7 copy-done.6
  2.5 0.1 broadcast_in_dim.50.kets_ref
  2.6 1.1 %copy-done = f32[2,1,2,96,384]{4,3,2,1,0:T(8,128)S(1)} copy-done((f32[2,1,2,96,384]{4,3,2,1,0:T(8,128)S(1)}, f32[2,1,2,96,384]{4,3,2,1,0:T(8,128)}, u32[]{:S(2)}) %copy-start) | copy-done | bytes 589848
  3.7 1.1 %copy-done.1 = f32[2,1,2,96,384]{4,3,2,1,0:T(8,128)S(1)} copy-done((f32[2,1,2,96,384]{4,3,2,1,0:T(8,128)S(1)}, f32[2,1,2,96,384]{4,3,2,1,0:T(8,128)}, u32[]{:S(2)}) %copy-start.1) | copy-done | bytes 589848
  4.7 1.0 copy-done.2
  5.7 1.0 copy-done.3
  6.7 60.8 %chains.1 = (f32[2,2,96,384]{3,2,1,0:T(8,128)S(1)}, f32[2,2,96,384]{3,2,1,0:T(8,128)S(1)}) custom-call(f32[2,2,32,128]{3,2,1,0:T(8,128)S(1)} %broadcast_in_dim.50.kets_ref, f32[2,2,96,384]{3,2,1,0:T(8,128)S(1)} %bitcast.13, f32[2,2,96,384]{3,2,1,0:T(8,128)S(1)} %bitcast.14, f32[2,96,384]{2,1,0:T(8,128)S(1)} %copy-done.2, f32[2,96,384]{2,1,0:T(8,128)S(1)} %copy-done.3), custom_call_target="tpu_custom_call" | custom-call | tf_op jit(solution)/shard_map/chains/pallas_call | solution.py:379
  67.5 0.0 copy-start.5
  67.5 0.0 copy-start.10
  67.6 0.1 broadcast_in_dim.52.kets_ref
  67.6 0.6 copy-done.10
  68.3 0.0 copy-done.7
  68.3 0.1 select_reduce_fusion
  68.4 0.6 copy-done.8
  69.1 0.1 broadcast_in_dim.53.rows_ref
  69.1 0.6 copy-done.9
  69.7 0.1 broadcast_in_dim.54.bonds_ref
  69.8 32.8 %environments.1 = f32[16,128]{1,0:T(8,128)S(1)} custom-call(f32[2,2,32,128]{3,2,1,0:T(8,128)S(1)} %broadcast_in_dim.52.kets_ref, f32[2,96,384]{2,1,0:T(8,128)S(1)} %get-tuple-element.8.above_ref, f32[2,96,384]{2,1,0:T(8,128)S(1)} %get-tuple-element.7.below_ref, f32[1,96,384]{2,1,0:T(8,128)S(1)} %copy-done.4, f32[1,96,384]{2,1,0:T(8,128)S(1)} %copy-done.5, ...), custom_call_target="tpu_custom_call" | custom-call | tf_op jit(solution)/shard_map/environments/pallas_call | solution.py:747
  102.6 0.6 slice_reduce_fusion
  103.2 0.9 fusion.2
  (16 shorter events, 0.1 us)
Async XLA Ops:
  1.8 0.7 copy-start.6
  2.6 1.1 %copy-start = (f32[2,1,2,96,384]{4,3,2,1,0:T(8,128)S(1)}, f32[2,1,2,96,384]{4,3,2,1,0:T(8,128)}, u32[]{:S(2)}) copy-start(f32[2,1,2,96,384]{4,3,2,1,0:T(8,128)} %param.12) | copy-start | bytes 1769476
  3.7 1.1 %copy-start.1 = (f32[2,1,2,96,384]{4,3,2,1,0:T(8,128)S(1)}, f32[2,1,2,96,384]{4,3,2,1,0:T(8,128)}, u32[]{:S(2)}) copy-start(f32[2,1,2,96,384]{4,3,2,1,0:T(8,128)} %param.13) | copy-start | bytes 1769476
  4.7 1.0 copy-start.2
  5.7 1.0 copy-start.3
  67.5 2.3 %copy-start.4 = (f32[1,96,384]{2,1,0:T(8,128)S(1)}, f32[1,96,384]{2,1,0:T(8,128)}, u32[]{:S(2)}) copy-start(f32[1,96,384]{2,1,0:T(8,128)} %left_ref.1) | copy-start | bytes 442372
  67.5 2.3 %copy-start.5 = (f32[1,96,384]{2,1,0:T(8,128)S(1)}, f32[1,96,384]{2,1,0:T(8,128)}, u32[]{:S(2)}) copy-start(f32[1,96,384]{2,1,0:T(8,128)} %right_ref.1) | copy-start | bytes 442372
  67.5 0.7 copy-start.10
  67.6 0.8 copy-start.7
  68.4 0.7 copy-start.8
  69.1 0.7 copy-start.9

commit v3 on v2

v3 whole, which is shorter than its diff:
```python
import functools

import jax
import jax.numpy as jnp
from jax import lax
from jax.experimental import pallas as pl
from jax.experimental.pallas import tpu as pltpu
from jax.sharding import PartitionSpec as P

D = 2
D2 = 4
PHYS = 2
EPSILON = 1e-06
LANES = 128


def unpack_lanes(tiles, chi):
    rolled = {}
    lane = lax.broadcasted_iota(jnp.int32, tiles[0].shape, 1)
    blocks = []
    for block in range(D2):
        total = jnp.zeros_like(tiles[0])
        for place, tile in enumerate(tiles):
            low = max(chi * block, LANES * place)
            high = min(chi * (block + 1), LANES * (place + 1))
            if low >= high:
                continue
            shift = (LANES * place - chi * block) % LANES
            if (place, shift) not in rolled:
                rolled[place, shift] = tile if shift == 0 else pltpu.roll(tile, shift, 1)
            inside = (lane >= low - chi * block) & (lane < high - chi * block)
            total = jnp.where(inside, rolled[place, shift], total)
        blocks.append(total)
    return blocks


def pack_lanes(blocks, chi):
    lane = lax.broadcasted_iota(jnp.int32, blocks[0].shape, 1)
    rolled = {}
    tiles = []
    for place in range(chi * D2 // LANES):
        total = jnp.zeros_like(blocks[0])
        for block, values in enumerate(blocks):
            low = max(chi * block, LANES * place)
            high = min(chi * (block + 1), LANES * (place + 1))
            if low >= high:
                continue
            shift = (chi * block - LANES * place) % LANES
            if (block, shift) not in rolled:
                rolled[block, shift] = values if shift == 0 else pltpu.roll(values, shift, 1)
            inside = (lane >= low - LANES * place) & (lane < high - LANES * place)
            total = jnp.where(inside, rolled[block, shift], total)
        tiles.append(total)
    return tiles


def halves(values):
    high = values.astype(jnp.bfloat16)
    low = (values - high.astype(jnp.float32)).astype(jnp.bfloat16)
    return high, low


def dot32(former, latter):
    return jnp.dot(former, latter, preferred_element_type=jnp.float32)


def dot_last(former, latter):
    return lax.dot_general(
        former, latter, (((1,), (1,)), ((), ())), preferred_element_type=jnp.float32
    )


def load_tiles(ref, at, width):
    return [ref[at, :, LANES * t : LANES * (t + 1)] for t in range(width // LANES)]


def window_kernel(
    row_count,
    col_count,
    kets_ref,
    left_maps_ref,
    right_maps_ref,
    top_ref,
    bottom_ref,
    left_ref,
    right_ref,
    rows_ref,
    bonds_ref,
    ops_ref,
    table_ref,
    out_ref,
    energy_ref,
    kets,
    kets_env,
    maps,
    edges,
    sides,
    env_ref,
    pbuf,
    qbuf,
    kbuf,
    xbuf,
    ebuf,
    pick,
    pboth,
    qhi,
    qlo,
    x32,
    jbuf,
    thi,
    tlo,
    near,
    far,
    vbuf,
    opens,
    hop_out,
    hop_in,
    half_in,
    shares,
    row_share,
    load_sem,
    map_send,
    map_recv,
    env_send,
    env_recv,
    out_send,
    out_recv,
    chain_send,
    chain_recv,
    hop_send,
    hop_recv,
    half_send,
    half_recv,
    share_send,
    share_recv,
):
    local_cols = kets.shape[1]
    chi, width = maps.shape[3], maps.shape[4]
    half = chi // 2
    wide = D2 * LANES
    pairs = PHYS * PHYS
    terms = rows_ref.shape[1]
    tall = shares.shape[1:]
    group = 2 * local_cols
    groups = row_count // group
    place = lax.axis_index("rows")
    cols_at = lax.axis_index("cols")
    has_left = cols_at > 0
    has_right = cols_at < col_count - 1
    mine = place // group
    me = place % group
    column = me // 2
    way = me % 2
    base = mine * group
    before = mine - 1 + 2 * way
    after = mine + 1 - 2 * way
    has_before = (before >= 0) & (before < groups)
    has_after = (after >= 0) & (after < groups)

    barrier = pltpu.get_barrier_semaphore()
    for other in range(row_count):

        @pl.when(place != other)
        def _():
            pl.semaphore_signal(barrier, inc=1, device_id={"rows": other})

    for other in range(col_count):

        @pl.when(cols_at != other)
        def _():
            pl.semaphore_signal(barrier, inc=1, device_id={"cols": other})

    loads = [
        pltpu.make_async_copy(source, target, load_sem.at[at])
        for at, (source, target) in enumerate(
            (
                (right_maps_ref.at[:, 0], maps.at[0]),
                (left_maps_ref.at[:, 0], maps.at[1]),
                (top_ref, edges.at[0]),
                (bottom_ref, edges.at[1]),
                (left_ref, sides.at[pl.ds(0, 1)]),
                (right_ref, sides.at[pl.ds(1, 1)]),
            )
        )
    ]
    for load in loads:
        load.start()

    count = kets_ref.shape[2]
    spot = lax.broadcasted_iota(jnp.int32, (count, count), 0)
    from_lane = lax.broadcasted_iota(jnp.int32, (count, count), 1)

    def exchanged(high, low):
        top, bottom = (spot // high) % 2, (spot // low) % 2
        return spot + (bottom - top) * high + (top - bottom) * low

    for order, target in ((spot, 0), (exchanged(8, 2), 1), (exchanged(4, 1), 2)):
        for at in range(local_cols):
            values = jnp.broadcast_to(kets_ref[0, at : at + 1, :], (count, count))
            tallest = jnp.sum(
                jnp.where(order == from_lane, values, 0.0), axis=1, keepdims=True
            )
            filled = jnp.broadcast_to(tallest, (count, LANES))
            if target < 2:
                kets[target, at] = filled
            if target != 1:
                kets_env[target // 2, at] = filled

    chosen = lax.broadcasted_iota(jnp.int32, (wide, width), 0)
    entry = lax.broadcasted_iota(jnp.int32, (wide, width), 1)
    wanted = (chosen % LANES) * D2 + chosen // LANES
    live = (chosen % LANES) < chi
    pick[...] = jnp.where((wanted == entry) & live, 1.0, 0.0).astype(jnp.bfloat16)
    thi[...] = jnp.zeros_like(thi)
    tlo[...] = jnp.zeros_like(tlo)
    for load in loads:
        load.wait()
    pl.semaphore_wait(barrier, row_count - 1 + col_count - 1)

    def map_copies(target_way, target_col, target, local):
        made = []
        for kind, (source, buffer) in enumerate(
            ((kets, kbuf), (maps.at[0], qbuf), (maps.at[1], pbuf))
        ):
            origin, landing = source.at[target_way, target_col], buffer.at[me]
            if local:
                made.append(pltpu.make_async_copy(origin, landing, map_recv.at[kind, me]))
            else:
                made.append(
                    pltpu.make_async_remote_copy(
                        origin,
                        landing,
                        map_send.at[kind, target],
                        map_recv.at[kind, me],
                        device_id={"rows": base + target},
                    )
                )
        return made

    low_half = jnp.where(mine >= groups // 2, 1, 0)
    for turn in range(group):
        target_way = (low_half + turn // local_cols) % 2
        target_col = turn % local_cols
        target = target_col * 2 + target_way

        @pl.when(target != me)
        def _():
            for copy in map_copies(target_way, target_col, target, False):
                copy.start()

        @pl.when(target == me)
        def _():
            for copy in map_copies(target_way, target_col, target, True):
                copy.start()

    def prepare(step, unused):
        slot = step + way * (group - 1 - 2 * step)
        for kind, buffer in enumerate((kbuf, qbuf, pbuf)):
            pltpu.make_async_copy(
                buffer.at[slot], buffer.at[slot], map_recv.at[kind, slot]
            ).wait()
        ket = kbuf[slot]
        half = ket.shape[0] // PHYS
        for i in range(half):
            total = ket[i : i + 1] * ket[0:half]
            for p in range(1, PHYS):
                total += ket[p * half + i : p * half + i + 1] * ket[p * half : (p + 1) * half]
            ebuf[step, i * half : (i + 1) * half] = total
        values = pick[...]
        for source, high_ref, low_ref, right in (
            (qbuf, qhi, qlo, True),
            (pbuf, pboth, pboth, False),
        ):
            for at, (part, ref) in enumerate(zip(halves(source[slot]), (high_ref, low_ref))):
                if right:
                    fill = jnp.zeros((LANES - chi, width), jnp.bfloat16)
                    tall = dot_last(values, jnp.concatenate([part, fill], axis=0))
                    for w in range(D2):
                        ref[step, :, w * LANES : (w + 1) * LANES] = tall[
                            w * LANES : (w + 1) * LANES
                        ].astype(jnp.bfloat16)
                else:
                    spread_map = dot_last(part, values).astype(jnp.bfloat16)
                    ref[step, at * chi : (at + 1) * chi] = spread_map
        return unused

    def row_copy(source, landing, send, recv, slot):
        remote = pltpu.make_async_remote_copy(
            source, landing, send, recv, device_id={"rows": base + slot}
        )
        return remote, pltpu.make_async_copy(source, landing, recv)

    def send_row(source, landing, send, recv, slot):
        remote, local = row_copy(source, landing, send, recv, slot)

        @pl.when(slot != me)
        def _():
            remote.start()

        @pl.when(slot == me)
        def _():
            local.start()

    chain_hop = pltpu.make_async_remote_copy(
        xbuf.at[group],
        xbuf.at[0],
        chain_send,
        chain_recv,
        device_id={"rows": after * group + me},
    )

    start_slot = way * (group - 1)
    crossing = jnp.logical_not(has_before) & ((start_slot // local_cols) != (me // local_cols))
    ahead = jnp.where(has_before, group, jnp.where(crossing, group - local_cols + 1, 1))
    turned_by = jnp.where(crossing, local_cols, 0)

    def prepare_ahead(turn, unused):
        return prepare((turn + turned_by) % group, unused)

    lax.fori_loop(0, ahead, prepare_ahead, 0)

    @pl.when(has_before)
    def _():
        pltpu.make_async_copy(xbuf.at[0], xbuf.at[0], chain_recv).wait()

    @pl.when(jnp.logical_not(has_before) & (way == 0))
    def _():
        xbuf[0] = edges[0, column]

    @pl.when(jnp.logical_not(has_before) & (way == 1))
    def _():
        xbuf[0] = edges[1, column]

    for u, block in enumerate(unpack_lanes(load_tiles(xbuf, 0, width), chi)):
        x32[u * chi : (u + 1) * chi] = block

    def absorb(step, unused):
        slot = step + way * (group - 1 - 2 * step)

        pending = (step >= 1) & jnp.logical_not(crossing & (step >= local_cols))

        @pl.when(pending & jnp.logical_not(has_before))
        def _():
            prepare(step, 0)

        send_row(
            xbuf.at[step], env_ref.at[way, column], env_send.at[step], env_recv.at[way, column], slot
        )
        x_high, x_low = halves(x32[...])
        q_high = qhi[step]
        jbuf[...] = dot32(x_high, q_high) + (dot32(x_high, qlo[step]) + dot32(x_low, q_high))
        chunk = 16

        def through(at, unused):
            start = pl.multiple_of(at * chunk, chunk)
            for l in range(D2):
                for d in range(D2):
                    total = None
                    for u in range(D2):
                        for w in range(D2):
                            ket_at = (u // D) * 8 + (l // D) * 4 + (d // D) * 2 + w // D
                            bra_at = (u % D) * 8 + (l % D) * 4 + (d % D) * 2 + w % D
                            spot = ket_at * 16 + bra_at
                            term = (
                                ebuf[step, spot : spot + 1, :]
                                * jbuf[
                                    pl.ds(u * chi + start, chunk), w * LANES : (w + 1) * LANES
                                ]
                            )
                            total = term if total is None else total + term
                    high, low = halves(total)
                    rows = pl.ds(l * LANES + start, chunk)
                    thi[rows, d * LANES : (d + 1) * LANES] = high
                    tlo[rows, d * LANES : (d + 1) * LANES] = low
            return unused

        lax.fori_loop(0, chi // chunk, through, 0)
        both = pboth[step]
        large = dot32(both, thi[:, 0:wide])
        renewed = large[:chi] + (large[chi:] + dot32(both[:chi], tlo[:, 0:wide]))
        square = jnp.sum(jnp.sum(renewed * renewed, axis=1, keepdims=True), axis=0, keepdims=True)
        renewed = renewed * (1.0 / jnp.sqrt(square / (chi * width) + EPSILON))
        blocks = [renewed[:, d * LANES : (d + 1) * LANES] for d in range(D2)]
        for d, block in enumerate(blocks):
            x32[d * chi : (d + 1) * chi] = block
        for t, tile in enumerate(pack_lanes(blocks, chi)):
            xbuf[step + 1, :, t * LANES : (t + 1) * LANES] = tile

        @pl.when((step == group - 1) & has_after)
        def _():
            chain_hop.start()

        send_row(
            xbuf.at[step + 1],
            out_ref.at[way, column],
            out_send.at[step],
            out_recv.at[way, column],
            slot,
        )
        return unused

    lax.fori_loop(0, group, absorb, 0)

    unit = jnp.where(
        lax.broadcasted_iota(jnp.int32, (LANES, LANES), 0)
        == lax.broadcasted_iota(jnp.int32, (LANES, LANES), 1),
        1.0,
        0.0,
    ).astype(jnp.bfloat16)
    fill = jnp.zeros((LANES - chi, LANES), jnp.bfloat16)

    def take_boundary(kind):
        for column in range(local_cols):
            landed = env_ref.at[kind, column]
            pltpu.make_async_copy(landed, landed, env_recv.at[kind, column]).wait()
            blocks = unpack_lanes(load_tiles(env_ref.at[kind], column, width), chi)
            for at, block in enumerate(blocks):
                lanes = slice(at * LANES, (at + 1) * LANES)
                for part, values in enumerate(halves(block)):
                    tall_block = jnp.concatenate([values, fill], axis=0)
                    turned = dot_last(unit, tall_block).astype(jnp.bfloat16)
                    if kind == 0:
                        rows = slice(part * chi, (part + 1) * chi)
                        near[0, column, rows, lanes] = turned[:chi]
                        near[1, column, rows, lanes] = values
                    else:
                        far[1, column, part, :, lanes] = turned
                        far[0, column, part, :, lanes] = tall_block

    for turn in range(2):
        for kind in range(2):

            @pl.when((turn + low_half) % 2 == kind)
            def _():
                take_boundary(kind)

    spot_row = lax.broadcasted_iota(jnp.int32, (terms, terms), 0)
    spot_lane = lax.broadcasted_iota(jnp.int32, (terms, terms), 1)

    def stand(ref):
        values = jnp.broadcast_to(ref[...].astype(jnp.float32), (terms, terms))
        return jnp.sum(jnp.where(spot_row == spot_lane, values, 0.0), axis=1, keepdims=True)

    term_row = stand(rows_ref).astype(jnp.int32)
    term_bond = stand(bonds_ref).astype(jnp.int32)
    term_op = stand(ops_ref).astype(jnp.int32)
    term_weights = jnp.zeros((terms, table_ref.shape[1]), jnp.float32)
    for op in range(table_ref.shape[0]):
        term_weights = jnp.where(term_op == op, table_ref[op : op + 1, :], term_weights)

    late = jnp.where(cols_at >= col_count // 2, 1, 0)

    def hop(side, step):
        return pltpu.make_async_remote_copy(
            hop_out.at[side],
            hop_in.at[side],
            hop_send.at[side],
            hop_recv.at[side],
            device_id={"cols": cols_at + step},
        )

    def half_copy(side):
        start, column, step = ((half, local_cols - 1, 1), (0, 0, -1))[side]
        return pltpu.make_async_remote_copy(
            opens.at[side, column, :, pl.ds(start, half)],
            half_in.at[side],
            half_send.at[side],
            half_recv.at[side],
            device_id={"cols": cols_at + step},
        )

    def put_environ(blocks):
        for at, block in enumerate(blocks):
            vbuf[at * chi : (at + 1) * chi] = block

    def walk(turn, unused):
        side = (turn // local_cols + late) % 2
        order = turn % local_cols
        column = order + side * (local_cols - 1 - 2 * order)
        first = ((side == 0) & (cols_at == 0)) | ((side == 1) & (cols_at == col_count - 1))
        final = ((side == 1) & (cols_at == 0)) | ((side == 0) & (cols_at == col_count - 1))
        ending = order == local_cols - 1

        @pl.when((order == 0) & jnp.logical_not(first))
        def _():
            pltpu.make_async_copy(hop_in.at[side], hop_in.at[side], hop_recv.at[side]).wait()
            put_environ(unpack_lanes(load_tiles(hop_in, side, width), chi))

        for at in range(2):

            @pl.when((order == 0) & first & (side == at))
            def _():
                put_environ(unpack_lanes(load_tiles(sides, at, width), chi))

        @pl.when(jnp.logical_not(ending & final))
        def _():
            v_high, v_low = halves(vbuf[...])
            f_high = far[side, column, 0]
            jbuf[...] = dot32(v_high, f_high) + (
                dot32(v_high, far[side, column, 1]) + dot32(v_low, f_high)
            )
            chunk = 16

            def ket(p, u, i, d, o):
                at = p * 16 + u * 8 + i * 4 + d * 2 + o
                return kets_env[side, column, at : at + 1, :]

            def through(at, unused):
                start = pl.multiple_of(at * chunk, chunk)

                def joined(i, d):
                    return jbuf[pl.ds(i * chi + start, chunk), d * LANES : (d + 1) * LANES]

                for p in range(PHYS):
                    for u in range(D):
                        for o in range(D):
                            part = {}
                            for i2 in range(D):
                                for d2 in range(D):
                                    total = None
                                    for i in range(D):
                                        for d in range(D):
                                            term = ket(p, u, i, d, o) * joined(
                                                i * D + i2, d * D + d2
                                            )
                                            total = term if total is None else total + term
                                    part[i2, d2] = total
                            for q in range(PHYS):
                                for u2 in range(D):
                                    for o2 in range(D):
                                        total = None
                                        for i2 in range(D):
                                            for d2 in range(D):
                                                term = ket(q, u2, i2, d2, o2) * part[i2, d2]
                                                total = term if total is None else total + term
                                        high, low = halves(total)
                                        rows = pl.ds((u * D + u2) * LANES + start, chunk)
                                        spot = (p * PHYS + q) * D2 + o * D + o2
                                        lanes = slice(spot * LANES, (spot + 1) * LANES)
                                        thi[rows, lanes] = high
                                        tlo[rows, lanes] = low
                return unused

            lax.fori_loop(0, chi // chunk, through, 0)
            both = near[side, column]
            wide = D2 * LANES
            closed = None
            for pair in range(pairs):
                lanes = slice(pair * wide, (pair + 1) * wide)
                large = dot32(both, thi[:, lanes])
                value = large[:chi] + (large[chi:] + dot32(both[:chi], tlo[:, lanes]))
                opens[side, column, pair] = value
                if pair // PHYS == pair % PHYS:
                    closed = value if closed is None else closed + value
            square = jnp.sum(
                jnp.sum(closed * closed, axis=1, keepdims=True), axis=0, keepdims=True
            )
            closed = closed * (1.0 / jnp.sqrt(square / (chi * width) + EPSILON))
            blocks = [closed[:, d * LANES : (d + 1) * LANES] for d in range(D2)]
            put_environ(blocks)

            @pl.when(ending)
            def _():
                for t, tile in enumerate(pack_lanes(blocks, chi)):
                    hop_out[side, :, t * LANES : (t + 1) * LANES] = tile

            for at, step in enumerate((1, -1)):

                @pl.when(ending & (side == at))
                def _():
                    hop(at, step).start()
                    half_copy(at).start()

        return unused

    lax.fori_loop(0, 2 * local_cols, walk, 0)

    lane = lax.broadcasted_iota(jnp.int32, tall, 1)

    def density(former, latter):
        total = jnp.zeros(tall, jnp.float32)
        for p in range(pairs):
            first = former(p)
            for q in range(pairs):
                value = jnp.sum(
                    jnp.sum(first * latter(q), axis=0, keepdims=True), axis=1, keepdims=True
                )
                total = jnp.where(lane == p * pairs + q, value, total)
        return total

    def share(bond, values):
        hit = (term_row == place) & (term_bond == bond)
        return jnp.where(hit, values, 0.0)

    held = shares.at[cols_at]
    held[...] = jnp.zeros(tall, jnp.float32)
    for column in range(local_cols - 1):
        held[...] += share(
            cols_at * local_cols + column,
            density(lambda p: opens[0, column, p], lambda q: opens[1, column + 1, q]),
        )

    def land(side):
        pltpu.make_async_copy(half_in.at[side], half_in.at[side], half_recv.at[side]).wait()

    @pl.when(has_right)
    def _():
        land(1)
        held[...] += share(
            cols_at * local_cols + local_cols - 1,
            density(lambda p: opens[0, local_cols - 1, p, :half], lambda q: half_in[1, q]),
        )

    @pl.when(has_left)
    def _():
        land(0)
        held[...] += share(
            cols_at * local_cols - 1,
            density(lambda p: half_in[0, p], lambda q: opens[1, 0, q, half:]),
        )

    def spread(buffer, stage, axis, at, count):
        def copies(other):
            return pltpu.make_async_remote_copy(
                buffer.at[at],
                buffer.at[at],
                share_send.at[stage, other],
                share_recv.at[stage, at],
                device_id={axis: other},
            )

        for other in range(count):

            @pl.when(at != other)
            def _():
                copies(other).start()

        for other in range(count):

            @pl.when(at != other)
            def _():
                pltpu.make_async_copy(
                    buffer.at[other], buffer.at[other], share_recv.at[stage, other]
                ).wait()

        total = buffer[0]
        for other in range(1, count):
            total += buffer[other]

        def finish():
            for other in range(count):

                @pl.when(at != other)
                def _():
                    copies(other).wait_send()

        return total, finish

    total, finish_cols = spread(shares, 0, "cols", cols_at, col_count)
    row_share[place] = total
    total, finish_rows = spread(row_share, 1, "rows", place, row_count)
    picked = jnp.sum(total[:, : pairs * pairs] * term_weights, axis=1, keepdims=True)
    bra, ket_at = lane % pairs, lane // pairs
    diagonal = (bra // PHYS == bra % PHYS) & (ket_at // PHYS == ket_at % PHYS)
    trace = jnp.sum(
        jnp.where(diagonal & (lane < pairs * pairs), total, 0.0), axis=1, keepdims=True
    )
    size = jnp.sqrt(jnp.sum(total * total, axis=1, keepdims=True))
    energy = picked / jnp.maximum(jnp.abs(trace), 0.25 * size)
    same = lax.broadcasted_iota(jnp.int32, (terms, terms), 0) == lax.broadcasted_iota(
        jnp.int32, (terms, terms), 1
    )
    energy_ref[...] = jnp.sum(jnp.where(same, energy, 0.0), axis=0, keepdims=True)
    finish_cols()
    finish_rows()

    @pl.when(has_right)
    def _():
        hop(0, 1).wait_send()
        half_copy(0).wait_send()

    @pl.when(has_left)
    def _():
        hop(1, -1).wait_send()
        half_copy(1).wait_send()

    for step in range(group):
        slot = step + way * (group - 1 - 2 * step)

        @pl.when(slot != me)
        def _():
            row_copy(
                xbuf.at[step],
                env_ref.at[way, column],
                env_send.at[step],
                env_recv.at[way, column],
                slot,
            )[0].wait_send()
            row_copy(
                xbuf.at[step + 1],
                out_ref.at[way, column],
                out_send.at[step],
                out_recv.at[way, column],
                slot,
            )[0].wait_send()

    for target in range(group):

        @pl.when(target != me)
        def _():
            for copy in map_copies(target % 2, target // 2, target, False):
                copy.wait_send()

    @pl.when(has_after)
    def _():
        chain_hop.wait_send()

    for a in range(2):
        for b in range(local_cols):
            pltpu.make_async_copy(out_ref.at[a, b], out_ref.at[a, b], out_recv.at[a, b]).wait()


def window(row_count, col_count, args):
    local_cols = args[0].shape[1]
    chi, width = args[1].shape[-2:]
    terms = args[7].shape[0]
    group = 2 * local_cols
    wide = D2 * LANES
    pairs = PHYS * PHYS
    most = max(row_count, col_count)
    entries = args[0].shape[2]
    vmem = pl.BlockSpec(memory_space=pltpu.VMEM)
    stay = pl.BlockSpec(memory_space=pltpu.HBM)
    dma = pltpu.SemaphoreType.DMA

    def f32(*shape):
        return pltpu.VMEM(shape, jnp.float32)

    def bf16(*shape):
        return pltpu.VMEM(shape, jnp.bfloat16)

    return pl.pallas_call(
        functools.partial(window_kernel, row_count, col_count),
        out_shape=(
            jax.ShapeDtypeStruct((2, local_cols, chi, width), jnp.float32),
            jax.ShapeDtypeStruct((1, terms), jnp.float32),
        ),
        in_specs=[vmem] + [stay] * 6 + [vmem] * 4,
        out_specs=(vmem, vmem),
        scratch_shapes=[
            f32(2, local_cols, entries, LANES),
            f32(2, local_cols, entries, LANES),
            f32(2, 2, local_cols, chi, width),
            f32(2, local_cols, chi, width),
            f32(2, chi, width),
            f32(2, local_cols, chi, width),
            f32(group, chi, width),
            f32(group, chi, width),
            f32(group, entries, LANES),
            f32(group + 1, chi, width),
            f32(group, D2**4, LANES),
            bf16(wide, width),
            bf16(group, 2 * chi, wide),
            bf16(group, LANES, wide),
            bf16(group, LANES, wide),
            f32(D2 * chi, LANES),
            f32(D2 * chi, wide),
            bf16(wide, pairs * wide),
            bf16(wide, pairs * wide),
            bf16(2, local_cols, 2 * chi, wide),
            bf16(2, local_cols, 2, LANES, wide),
            f32(D2 * chi, LANES),
            f32(2, local_cols, pairs, chi, wide),
            f32(2, chi, width),
            f32(2, chi, width),
            f32(2, pairs, chi // 2, wide),
            f32(col_count, terms, LANES),
            f32(row_count, terms, LANES),
            dma((6,)),
            dma((3, group)),
            dma((3, group)),
            dma((group,)),
            dma((2, local_cols)),
            dma((group,)),
            dma((2, local_cols)),
            dma,
            dma,
            dma((2,)),
            dma((2,)),
            dma((2,)),
            dma((2,)),
            dma((2, most)),
            dma((2, most)),
        ],
        compiler_params=pltpu.CompilerParams(
            collective_id=0, has_side_effects=True, vmem_limit_bytes=56 * 1024 * 1024
        ),
        name="window",
    )(*args[:7], *(index[None] for index in args[7:10]), args[10])


def shards(*args):
    outs, energies = window(lax.axis_size("rows"), lax.axis_size("cols"), args)
    return (outs[0][None], outs[1][None], energies[0])


def solution(mesh):
    placed = (
        P("rows", "cols", None),
        P(None, "rows", "cols", None, None),
        P(None, "rows", "cols", None, None),
        P("cols", None, None),
        P("cols", None, None),
        P("rows", None, None),
        P("rows", None, None),
        P(),
        P(),
        P(),
        P(),
    )
    return jax.shard_map(
        shards,
        mesh=mesh,
        in_specs=placed,
        out_specs=(P("rows", "cols", None, None), P("rows", "cols", None, None), P()),
        check_vma=False,
    )
```

time: 104 us -> 97.3 us (0.936)
  local copies, waits for them, and re-layouts: 9.63 us -> 3.01 us
    unnamed x22 -> x3, local copies, waits for them, and re-layouts: 6.64 us -> 1.1 us
    pallas_call x2 -> x1, Pallas kernels: 93.6 us -> 93.5 us  [window(): pl.pallas_call(functools.partial(window_kernel, row_count, col_count), ou...]
where the time goes in v3:
time: 97.3 us; the launch traced here: 97.1 us
  Pallas kernels  93.5 us (96%)
  local copies, waits for them, and re-layouts  3.01 us (3%)
    pallas_call x1, Pallas kernels, window(): pl.pallas_call(functools.partial(window_kernel, row_count, col_count), ou...  93.5 us

profile of v3, /device:TPU:0, one launch (start us, length us, event | category | flops | bytes accessed | tf_op | source)
XLA Modules:
  0.0 97.1 jit_solution(10331442013990183027)
XLA Ops:
  0.6 93.5 %window.1 = (f32[2,2,96,384]{3,2,1,0:T(8,128)}, f32[1,16]{1,0:T(1,128)}) custom-call(f32[1,2,32]{2,1,0:T(2,128)} %kets_ref.1, f32[2,1,2,96,384]{4,3,2,1,0:T(8,128)} %left_maps_ref.1, f32[2,1,2,96,384]{4,3,2,1,0:T(8,128)} %right_maps_ref.1, f32[2,96,384]{2,1,0:T(8,128)} %top_ref.1, f32[2,96,384]{2,1,0:T(8,128)} %bottom_ref.1, f32[1,96,384]{2,1,0:T(8,128)} %left_ref.1, ...), custom_call_target="tpu_custom_call" | custom-call | tf_op jit(solution)/shard_map/window/pallas_call | solution.py:742
  94.1 1.9 %fusion = (f32[1,2,96,384]{3,2,1,0:T(8,128)}, f32[1,2,96,384]{3,2,1,0:T(8,128)}) fusion(f32[2,2,96,384]{3,2,1,0:T(8,128)} %get-tuple-element.5), kind=kLoop, calls=%fused_computation | loop fusion | bytes 1179648 | tf_op jit(solution)/shard_map/slice | solution.py:804
  96.0 0.0 copy-start
  96.0 0.6 copy-done
  96.6 0.5 copy.15
Async XLA Ops:
  96.0 0.6 copy-start
